TPU v7x, 32 devices: a whole 2x2x4 slice. The times are simulated.
32 devices in a mesh: ex: 4 (over y, x), ey: 2 (over core), tp: 4 (over z).
Axes of the slice: x: 2, y: 2, z: 4, core: 2. Of those that a mesh axis runs over, the one named last changes fastest.
Arguments:
- tokens: bfloat16 [256, 7168], P(('ex', 'ey'), 'tp'), may hold values from -6 to 6
- cotangent: bfloat16 [256, 7168], P(('ex', 'ey'), 'tp'), may hold values from -0.59765625 to 0.59765625
- gates: bfloat16 [256, 8], P(('ex', 'ey')), may hold values from 0.049804688 to 1
- expert_ids: int32 [256, 8], P(('ex', 'ey')), may hold values from 0 to 31, all different within a row; in each aligned block of 32 rows (0 to 31, 32 to 63, ...) at most 10 rows name the same one
- saved_gate: bfloat16 [1024, 32, 80], P(None, ('ex', 'ey')), may hold values from -6 to 6
- saved_up: bfloat16 [1024, 32, 80], P(None, ('ex', 'ey')), may hold values from -6 to 6
- w_gate: bfloat16 [32, 7168, 1024], P(('ex', 'ey'), 'tp'), may hold values from -0.1875 to 0.1875
- w_up: bfloat16 [32, 7168, 1024], P(('ex', 'ey'), 'tp'), may hold values from -0.1875 to 0.1875
- w_down: bfloat16 [32, 1024, 7168], P(('ex', 'ey'), None, 'tp'), may hold values from -0.25 to 0.25
Outputs:
- grad_tokens: bfloat16 [256, 7168], P(('ex', 'ey'), 'tp')
- grad_gates: bfloat16 [256, 8], P(('ex', 'ey'))
- grad_w_gate: bfloat16 [32, 7168, 1024], P(('ex', 'ey'), 'tp')
- grad_w_up: bfloat16 [32, 7168, 1024], P(('ex', 'ey'), 'tp')
- grad_w_down: bfloat16 [32, 1024, 7168], P(('ex', 'ey'), None, 'tp')
Inputs may be any that keep to these rules, and one draw needn't show every extreme that they name: `expert_ids`: each row names 8 different experts. The rows of one token group name any one expert at most 10 times, a bound that some block reaches.
All inputs are finite; a program needn't handle non-finite values.
Results may differ from a plain program's by a relative error of at most 0.025.
Values may be sent and summed in bfloat16 or wider, within the bound.
A program may use at most 128 MiB of HBM per device.

v0:
```python
import jax
import jax.numpy as jnp
from jax import lax
from jax.sharding import PartitionSpec as P

LANES = 128
GROUP = ("ex", "ey")


def scatter_blocks(blocks, parts):
    if parts > 4:
        got = lax.all_to_all(blocks, "tp", split_axis=0, concat_axis=0, tiled=True)
        return [got[i] for i in range(parts)]
    me = lax.axis_index("tp")
    got = [lax.dynamic_index_in_dim(blocks, me, 0, keepdims=False)]
    for step in range(1, parts):
        piece = lax.dynamic_index_in_dim(blocks, (me + step) % parts, 0, keepdims=False)
        got.append(lax.ppermute(piece, "tp", [(i, (i + step) % parts) for i in range(parts)]))
    return got


def block_sum(terms):
    return sum(term.astype(jnp.float32) for term in terms).astype(jnp.bfloat16)


def gather_pieces(block, parts):
    if parts > 4:
        return [lax.all_gather(block, "tp", axis=0)]
    shifts = [[(i, (i + step) % parts) for i in range(parts)] for step in range(1, parts)]
    return [block] + [lax.ppermute(block, "tp", shift) for shift in shifts]


def in_order(pieces, parts):
    if parts > 4:
        return pieces[0]
    me = lax.axis_index("tp")
    whole = jnp.zeros((parts,) + pieces[0].shape, pieces[0].dtype)
    for step, piece in enumerate(pieces):
        whole = lax.dynamic_update_index_in_dim(whole, piece, (me - step) % parts, 0)
    return whole


def on_device(tokens, cotangent, gates, expert_ids, saved_gate, saved_up, w_gate, w_up, w_down):
    groups = lax.axis_size(GROUP)
    parts = lax.axis_size("tp")
    rows, width = tokens.shape
    top = expert_ids.shape[1]
    hidden_units, local, slots = saved_gate.shape
    capacity = slots // groups
    total = groups * rows
    first = lax.axis_index(GROUP) * local

    extra = jnp.concatenate(
        [gates, expert_ids.astype(jnp.bfloat16), jnp.zeros((rows, LANES - 2 * top), jnp.bfloat16)],
        axis=1,
    )
    packed = jnp.concatenate([cotangent, extra], axis=1)
    packed = lax.all_gather(packed, GROUP, axis=0, tiled=True)
    tokens, packed = lax.optimization_barrier((tokens, packed))
    all_x = lax.all_to_all(
        jnp.broadcast_to(tokens[None], (groups, rows, width)),
        GROUP, split_axis=0, concat_axis=0, tiled=True,
    ).reshape(total, width)
    all_dy = packed[:, :width]
    small = packed[:, width:].astype(jnp.float32).T
    all_gates = small[:top]
    all_ids = small[top : 2 * top].astype(jnp.int32)

    match = all_ids[None] == first + jnp.arange(local, dtype=jnp.int32)[:, None, None]
    named = jnp.sum(match.astype(jnp.float32), axis=1)
    gate_of = jnp.sum(jnp.where(match, all_gates[None], 0.0), axis=1)
    place = jnp.arange(total, dtype=jnp.int32)
    group_of = place // rows
    earlier = (place[:, None] < place[None, :]) & (group_of[:, None] == group_of[None, :])
    position = jnp.dot(
        named.astype(jnp.bfloat16), earlier.astype(jnp.bfloat16), preferred_element_type=jnp.float32
    ).astype(jnp.int32)
    row_of = jnp.where(named > 0, group_of[None] * capacity + position, -1)
    taken = row_of[:, None, :] == jnp.arange(slots, dtype=jnp.int32)[None, :, None]
    chosen = taken.astype(jnp.bfloat16).reshape(local * slots, total)
    gate_rows = jnp.sum(jnp.where(taken, gate_of[:, None, :], 0.0), axis=2, keepdims=True)

    dy_rows = jnp.dot(chosen, all_dy, preferred_element_type=jnp.float32).astype(jnp.bfloat16)
    dy_rows = dy_rows.reshape(local, slots, width)
    halves = 2 if local % 2 == 0 else 1
    each = local // halves
    cuts = [slice(h * each, (h + 1) * each) for h in range(halves)]
    received = []
    for cut in cuts:
        raw = jnp.einsum(
            "erd,efd->erf", dy_rows[cut], w_down[cut], preferred_element_type=jnp.float32
        ).astype(jnp.bfloat16)
        raw = raw.reshape(parts, each * slots // parts, hidden_units)
        received.append(scatter_blocks(raw, parts))

    scaled = (gate_rows * dy_rows.astype(jnp.float32)).astype(jnp.bfloat16)
    act_gate = saved_gate.transpose(1, 2, 0).astype(jnp.float32)
    act_up = saved_up.transpose(1, 2, 0).astype(jnp.float32)
    sigm = jax.nn.sigmoid(act_gate)
    hidden = (act_gate * sigm * act_up).astype(jnp.bfloat16)
    sums = [block_sum(received[0])]
    hidden, scaled, sums[0] = lax.optimization_barrier((hidden, scaled, sums[0]))
    grad_w_down = jnp.einsum(
        "erf,erd->efd", hidden, scaled, preferred_element_type=jnp.float32
    ).astype(jnp.bfloat16)

    for terms in received[1:]:
        terms, grad_w_down = lax.optimization_barrier((terms, grad_w_down))
        sums.append(block_sum(terms))
    gathered = [gather_pieces(block, parts) for block in sums]
    d_gate, d_up, score, dx_rows = [], [], [], []
    for cut, pieces in zip(cuts, gathered):
        if dx_rows:
            pieces, dx_rows[-1] = lax.optimization_barrier((pieces, dx_rows[-1]))
        raw = in_order(pieces, parts).reshape(each, slots, hidden_units).astype(jnp.float32)
        a, u, q = act_gate[cut], act_up[cut], sigm[cut]
        dh = gate_rows[cut] * raw
        part_score = jnp.sum(raw * hidden[cut].astype(jnp.float32), axis=2, keepdims=True)
        part_gate = (dh * u * q * (1.0 + a * (1.0 - q))).astype(jnp.bfloat16)
        part_up = (dh * a * q).astype(jnp.bfloat16)
        part_gate, part_up = lax.optimization_barrier((part_gate, part_up))
        dx = jnp.einsum("erf,edf->erd", part_gate, w_gate[cut], preferred_element_type=jnp.float32)
        dx = dx + jnp.einsum("erf,edf->erd", part_up, w_up[cut], preferred_element_type=jnp.float32)
        dx_rows.append(dx.astype(jnp.bfloat16))
        d_gate.append(part_gate)
        d_up.append(part_up)
        score.append(part_score)
    d_gate, d_up, score, dx_rows = [
        jnp.concatenate(pieces, axis=0) for pieces in (d_gate, d_up, score, dx_rows)
    ]
    dx_rows = dx_rows.reshape(local * slots, width)
    own = jnp.arange(LANES)[None, None, :] == jnp.arange(local)[:, None, None]
    score_cols = jnp.where(own, score, 0.0).astype(jnp.bfloat16).reshape(local * slots, LANES)
    over_rows = (((0,), (0,)), ((), ()))
    back = [
        lax.dot_general(chosen, part, over_rows, preferred_element_type=jnp.float32).astype(
            jnp.bfloat16
        )
        for part in (dx_rows, score_cols)
    ]
    back = jnp.concatenate(back, axis=1).reshape(groups, rows, width + LANES)
    back = lax.all_to_all(back, GROUP, split_axis=0, concat_axis=0, tiled=True)

    x_rows = jnp.dot(chosen, all_x, preferred_element_type=jnp.float32).astype(jnp.bfloat16)
    x_rows = x_rows.reshape(local, slots, width)
    grad_w_gate = jnp.einsum(
        "erd,erf->edf", x_rows, d_gate, preferred_element_type=jnp.float32
    ).astype(jnp.bfloat16)
    grad_w_up = jnp.einsum(
        "erd,erf->edf", x_rows, d_up, preferred_element_type=jnp.float32
    ).astype(jnp.bfloat16)

    grad_tokens = jnp.sum(back[:, :, :width].astype(jnp.float32), axis=0).astype(jnp.bfloat16)
    table = back[:, :, width : width + local].transpose(1, 0, 2).reshape(rows, groups * local)
    picks = expert_ids[:, :, None] == jnp.arange(groups * local, dtype=jnp.int32)[None, None, :]
    grad_gates = jnp.sum(
        jnp.where(picks, table.astype(jnp.float32)[:, None, :], 0.0), axis=2
    ).astype(jnp.bfloat16)
    return (grad_tokens, grad_gates, grad_w_gate, grad_w_up, grad_w_down)


def solution(mesh):
    by_group = P(GROUP, "tp")
    small = P(GROUP, None)
    saved = P(None, GROUP, None)
    wide = P(GROUP, "tp", None)
    down = P(GROUP, None, "tp")
    in_specs = (by_group, by_group, small, small, saved, saved, wide, wide, down)
    out_specs = (by_group, small, wide, wide, down)
    return jax.shard_map(
        on_device, mesh=mesh, in_specs=in_specs, out_specs=out_specs, check_vma=False
    )
```

profile of v0, /device:TPU:0, one launch (start us, length us, event | category | flops | bytes accessed | tf_op | source)
XLA Modules:
  0.0 115.9 jit_solution(15923478106026008111)
XLA Ops:
  0.6 0.8 copy.58
  1.4 0.8 copy.57
  2.2 1.0 concatenate.18
  3.2 12.3 %all_gather.3 = bf16[256,1920]{1,0:T(8,128)(2,1)S(1)} all-gather(bf16[32,1920]{1,0:T(8,128)(2,1)S(1)} %concatenate.18), channel_id=1, replica_groups=mesh['ex'=4,'ey'=2,'tp'=4] {'ex','ey'}, dimensions={0}, use_global_device_ids=true | all-gather | bytes 1105920 | tf_op jit(solution)/shard_map/all_gather | solution.py:58
  15.5 1.0 broadcast_in_dim.141
  16.5 4.2 %all-to-all-start.1 = ((bf16[8,32,1792]{2,1,0:T(8,128)(2,1)}), bf16[8,32,1792]{2,1,0:T(8,128)(2,1)}, u32[]{:S(2)}, u32[]{:S(2)}) async-start(bf16[8,32,1792]{2,1,0:T(8,128)(2,1)} %broadcast_in_dim.141), calls=%async_computation.1 | async-start | bytes 1835008 | tf_op jit(solution)/shard_map/all_to_all | solution.py:60
  20.9 0.6 copy.59
  21.7 0.2 fusion.37
  22.1 0.5 convolution_convert_fusion.4
  22.6 5.4 %fusion.26 = bf16[2,80,1024]{2,1,0:T(8,128)(2,1)S(1)} fusion(bf16[2,80,1792]{2,1,0:T(8,128)(2,1)S(1)} %bitcast.106, bf16[4,1024,1792]{2,1,0:T(8,128)(2,1)} %param.17), kind=kOutput, calls=%fused_computation.29 | convolution fusion | flops 587366400 | bytes 8241152 | tf_op jit(solution)/shard_map/erd,efd->erf/dot_general | solution.py:90
  28.1 0.7 dynamic-slice_bitcast_fusion.3
  28.8 3.6 %collective-permute-start.2 = (bf16[40,1024]{1,0:T(8,128)(2,1)}, bf16[40,1024]{1,0:T(8,128)(2,1)}, u32[]{:S(2)}, u32[]{:S(2)}) collective-permute-start(bf16[40,1024]{1,0:T(8,128)(2,1)} %get-tuple-element.77), channel_id=1, source_target_pairs={{0,3},{1,0},{2,1},{3,2},{4,7},{5,4},{6,5},{7,6},{8,11},{9,8},{10,9... | collective-permute-start | bytes 245768 | tf_op jit(solution)/shard_map/ppermute | solution.py:18
  32.4 5.5 %fusion.29 = bf16[2,80,1024]{2,1,0:T(8,128)(2,1)S(1)} fusion(bf16[2,80,1792]{2,1,0:T(8,128)(2,1)S(1)} %bitcast.105, bf16[4,1024,1792]{2,1,0:T(8,128)(2,1)} %param.17), kind=kOutput, calls=%fused_computation.30 | convolution fusion | flops 587366400 | bytes 8241152 | tf_op jit(solution)/shard_map/erd,efd->erf/dot_general | solution.py:90
  37.9 0.7 dynamic-slice_bitcast_fusion.2
  38.6 1.0 collective-permute-start.3
  39.6 2.8 %collective-permute-start.5 = (bf16[40,1024]{1,0:T(8,128)(2,1)}, bf16[40,1024]{1,0:T(8,128)(2,1)}, u32[]{:S(2)}, u32[]{:S(2)}) collective-permute-start(bf16[40,1024]{1,0:T(8,128)(2,1)} %get-tuple-element.82), channel_id=1, source_target_pairs={{0,3},{1,0},{2,1},{3,2},{4,7},{5,4},{6,5},{7,6},{8,11},{9,8},{10,9... | collective-permute-start | bytes 245768 | tf_op jit(solution)/shard_map/ppermute | solution.py:18
  42.4 1.1 collective-permute-start.4
  43.6 1.5 %add_divide_fusion = (f32[4,80,1024]{2,1,0:T(8,128)}, bf16[4,80,1024]{2,1,0:T(8,128)(2,1)S(1)}) fusion(bf16[1024,4,80]{0,2,1:T(8,128)(2,1)S(1)} %copy-done.4, bf16[1024,4,80]{0,2,1:T(8,128)(2,1)S(1)} %copy-done.3), kind=kLoop, calls=%fused_computation.28 | loop fusion | flops 2621440 | bytes 3276800 | tf_op jit(solution)/shard_map/div | solution.py:99
  45.2 1.8 %convert_bitcast_fusion = (f32[4,80,1024]{2,1,0:T(8,128)}, f32[4,80,1024]{2,1,0:T(8,128)}) fusion(bf16[1024,4,80]{0,2,1:T(8,128)(2,1)S(1)} %copy-done.3, bf16[1024,4,80]{0,2,1:T(8,128)(2,1)S(1)} %copy-done.4), kind=kLoop, calls=%fused_computation.25 | loop fusion | flops 655360 | bytes 3932160 | tf_op jit(solution)/shard_map/convert_element_type | solution.py:98
  47.0 0.1 select_reduce_fusion
  47.1 0.3 fusion.25
  47.4 1.3 %collective-permute-start = (bf16[40,1024]{1,0:T(8,128)(2,1)}, bf16[40,1024]{1,0:T(8,128)(2,1)S(1)}, u32[]{:S(2)}, u32[]{:S(2)}) collective-permute-start(bf16[40,1024]{1,0:T(8,128)(2,1)} %get-tuple-element.79), channel_id=1, source_target_pairs={{0,1},{1,2},{2,3},{3,0},{4,5},{5,6},{6,7},{7,4},{8,9},{9,10},{10,1... | collective-permute-start | bytes 245768 | tf_op jit(solution)/shard_map/ppermute | solution.py:18
  48.7 1.6 %collective-permute-done.4 = bf16[40,1024]{1,0:T(8,128)(2,1)} collective-permute-done((bf16[40,1024]{1,0:T(8,128)(2,1)}, bf16[40,1024]{1,0:T(8,128)(2,1)}, u32[]{:S(2)}, u32[]{:S(2)}) %collective-permute-start.4) | collective-permute-done | bytes 81952 | tf_op jit(solution)/shard_map/ppermute | solution.py:18
  50.4 1.0 fusion.66
  51.4 2.2 %collective-permute-start.11 = (bf16[40,1024]{1,0:T(8,128)(2,1)S(1)}, bf16[40,1024]{1,0:T(8,128)(2,1)S(1)}, u32[]{:S(2)}, u32[]{:S(2)}) collective-permute-start(bf16[40,1024]{1,0:T(8,128)(2,1)S(1)} %fusion.66), channel_id=1, source_target_pairs={{0,3},{1,0},{2,1},{3,2},{4,7},{5,4},{6,5},{7,6},{8,11},{9,8},{10,9... | collective-permute-start | bytes 245768 | tf_op jit(solution)/shard_map/ppermute | solution.py:30
  53.8 7.6 %convolution_convert_fusion.2 = bf16[4,1024,1792]{2,1,0:T(8,128)(2,1)} fusion(bf16[4,80,1024]{2,1,0:T(8,128)(2,1)S(1)} %get-tuple-element.25, bf16[4,80,1792]{2,1,0:T(8,128)(2,1)S(1)} %fusion.25), kind=kOutput, calls=%fused_computation.2 | convolution fusion | flops 1181745152 | bytes 16482304 | tf_op jit(solution)/shard_map/erf,erd->efd/dot_general | solution.py:103
  61.3 0.5 collective-permute-start.9
  61.9 1.0 add_convert_fusion
  62.9 3.4 %collective-permute-start.8 = (bf16[40,1024]{1,0:T(8,128)(2,1)S(1)}, bf16[40,1024]{1,0:T(8,128)(2,1)S(1)}, u32[]{:S(2)}, u32[]{:S(2)}) collective-permute-start(bf16[40,1024]{1,0:T(8,128)(2,1)S(1)} %add_convert_fusion), channel_id=1, source_target_pairs={{0,3},{1,0},{2,1},{3,2},{4,7},{5,4},{6,5},{7,6},{8,11},{9,8},{10,9... | collective-permute-start | bytes 245768 | tf_op jit(solution)/shard_map/ppermute | solution.py:30
  66.2 1.0 collective-permute-start.7
  67.3 1.3 %collective-permute-done.9 = bf16[40,1024]{1,0:T(8,128)(2,1)S(1)} collective-permute-done((bf16[40,1024]{1,0:T(8,128)(2,1)S(1)}, bf16[40,1024]{1,0:T(8,128)(2,1)S(1)}, u32[]{:S(2)}, u32[]{:S(2)}) %collective-permute-start.9) | collective-permute-done | bytes 81952 | tf_op jit(solution)/shard_map/ppermute | solution.py:30
  68.5 2.4 %collective-permute-start.6 = (bf16[40,1024]{1,0:T(8,128)(2,1)S(1)}, bf16[40,1024]{1,0:T(8,128)(2,1)S(1)}, u32[]{:S(2)}, u32[]{:S(2)}) collective-permute-start(bf16[40,1024]{1,0:T(8,128)(2,1)S(1)} %add_convert_fusion), channel_id=1, source_target_pairs={{0,1},{1,2},{2,3},{3,0},{4,5},{5,6},{6,7},{7,4},{8,9},{9,10},{10,1... | collective-permute-start | bytes 245768 | tf_op jit(solution)/shard_map/ppermute | solution.py:30
  71.0 0.4 fusion.52
  71.4 5.6 %fusion.4 = f32[2,80,1792]{2,1,0:T(8,128)S(1)} fusion(bf16[2,80,1024]{2,1,0:T(8,128)(2,1)S(1)} %get-tuple-element.33, bf16[4,1792,1024]{2,1,0:T(8,128)(2,1)} %param.16), kind=kOutput, calls=%fused_computation.7 | convolution fusion | flops 587202560 | bytes 8814592 | tf_op jit(solution)/shard_map/erf,edf->erd/dot_general | solution.py:123
  77.0 5.6 %fusion.22 = bf16[2,80,1792]{2,1,0:T(8,128)(2,1)S(1)} fusion(f32[2,80,1792]{2,1,0:T(8,128)S(1)} %fusion.4, bf16[2,80,1024]{2,1,0:T(8,128)(2,1)S(1)} %get-tuple-element.32, bf16[4,1792,1024]{2,1,0:T(8,128)(2,1)} %param.15), kind=kOutput, calls=%fused_computation.22 | convolution fusion | flops 587776000 | bytes 9388032 | tf_op jit(solution)/shard_map/erf,edf->erd/dot_general | solution.py:122
  82.8 0.6 fusion.47
  83.3 5.6 %fusion = f32[2,80,1792]{2,1,0:T(8,128)S(1)} fusion(bf16[2,80,1024]{2,1,0:T(8,128)(2,1)S(1)} %get-tuple-element.40, bf16[4,1792,1024]{2,1,0:T(8,128)(2,1)} %param.16), kind=kOutput, calls=%fused_computation.3 | convolution fusion | flops 587202560 | bytes 8814592 | tf_op jit(solution)/shard_map/erf,edf->erd/dot_general | solution.py:123
  89.0 2.4 %fusion.19 = bf16[2,80,1792]{2,1,0:T(8,128)(2,1)S(1)} fusion(f32[2,80,1792]{2,1,0:T(8,128)S(1)} %fusion, bf16[2,80,1024]{2,1,0:T(8,128)(2,1)S(1)} %get-tuple-element.39, bf16[4,1792,1024]{2,1,0:T(8,128)(2,1)S(1)} %bitcast.115), kind=kOutput, calls=%fused_computation.21 | convolution fusion | flops 587776000 | bytes 9388032 | tf_op jit(solution)/shard_map/erf,edf->erd/dot_general | solution.py:122
  91.3 0.4 fusion.35
  91.7 0.7 fusion.12
  92.4 1.0 pad_maximum_fusion
  93.4 3.8 %all-to-all-start = ((bf16[8,32,1920]{2,1,0:T(8,128)(2,1)}), bf16[8,32,1920]{2,1,0:T(8,128)(2,1)S(1)}, u32[]{:S(2)}, u32[]{:S(2)}) async-start(bf16[8,32,1920]{2,1,0:T(8,128)(2,1)} %bitcast.34), calls=%async_computation | async-start | bytes 1966080 | tf_op jit(solution)/shard_map/all_to_all | solution.py:142
  97.3 1.6 %convolution_convert_fusion.3 = bf16[320,1792]{1,0:T(8,128)(2,1)S(1)} fusion(pred[320,256]{1,0:T(8,128)(4,1)S(1)} %bitcast.107, bf16[256,1792]{1,0:T(8,128)(2,1)} %bitcast.38), kind=kOutput, calls=%fused_computation.16 | convolution fusion | flops 294174720 | bytes 2146304 | tf_op jit(solution)/shard_map/dot_general | solution.py:144
  98.9 7.6 %convolution_convert_fusion.1 = bf16[4,1792,1024]{2,1,0:T(8,128)(2,1)} fusion(bf16[4,80,1792]{2,1,0:T(8,128)(2,1)S(1)} %bitcast.99, bf16[2,80,1024]{2,1,0:T(8,128)(2,1)S(1)} %get-tuple-element.39, bf16[2,80,1024]{2,1,0:T(8,128)(2,1)S(1)} %get-tuple-element.32), kind=kOutput, calls=%fused_computation.1 | convolution fusion | flops 1182072832 | bytes 16482304 | tf_op jit(solution)/shard_map/erd,erf->edf/dot_general | solution.py:146
  106.5 7.6 %convolution_convert_fusion = bf16[4,1792,1024]{2,1,0:T(8,128)(2,1)} fusion(bf16[4,80,1792]{2,1,0:T(8,128)(2,1)S(1)} %bitcast.100, bf16[2,80,1024]{2,1,0:T(8,128)(2,1)S(1)} %get-tuple-element.40, bf16[2,80,1024]{2,1,0:T(8,128)(2,1)S(1)} %get-tuple-element.33), kind=kOutput, calls=%fused_computation | convolution fusion | flops 1182072832 | bytes 16482304 | tf_op jit(solution)/shard_map/erd,erf->edf/dot_general | solution.py:149
  114.3 0.2 select_reduce_fusion.1
  114.5 0.7 copy.66
  115.2 0.8 slice_reduce_fusion
  (65 shorter events, 1.0 us)
Async XLA Ops:
  0.6 14.9 %copy-start.6 = (bf16[32,1792]{1,0:T(8,128)(2,1)S(1)}, bf16[32,1792]{1,0:T(8,128)(2,1)}, u32[]{:S(2)}) copy-start(bf16[32,1792]{1,0:T(8,128)(2,1)} %param.9) | copy-start | bytes 344068
  16.5 76.9 %all-to-all-start.1 = ((bf16[8,32,1792]{2,1,0:T(8,128)(2,1)}), bf16[8,32,1792]{2,1,0:T(8,128)(2,1)}, u32[]{:S(2)}, u32[]{:S(2)}) async-start(bf16[8,32,1792]{2,1,0:T(8,128)(2,1)} %broadcast_in_dim.141), calls=%async_computation.1 | async-start | bytes 1835008 | tf_op jit(solution)/shard_map/all_to_all | solution.py:60
  28.8 32.6 %collective-permute-start.2 = (bf16[40,1024]{1,0:T(8,128)(2,1)}, bf16[40,1024]{1,0:T(8,128)(2,1)}, u32[]{:S(2)}, u32[]{:S(2)}) collective-permute-start(bf16[40,1024]{1,0:T(8,128)(2,1)} %get-tuple-element.77), channel_id=1, source_target_pairs={{0,3},{1,0},{2,1},{3,2},{4,7},{5,4},{6,5},{7,6},{8,11},{9,8},{10,9... | collective-permute-start | bytes 245768 | tf_op jit(solution)/shard_map/ppermute | solution.py:18
  32.4 29.5 %collective-permute-start.1 = (bf16[40,1024]{1,0:T(8,128)(2,1)}, bf16[40,1024]{1,0:T(8,128)(2,1)}, u32[]{:S(2)}, u32[]{:S(2)}) collective-permute-start(bf16[40,1024]{1,0:T(8,128)(2,1)} %get-tuple-element.78), channel_id=1, source_target_pairs={{0,2},{1,3},{2,0},{3,1},{4,6},{5,7},{6,4},{7,5},{8,10},{9,11},{10,... | collective-permute-start | bytes 245768 | tf_op jit(solution)/shard_map/ppermute | solution.py:18
  32.4 11.2 %copy-start.3 = (bf16[1024,4,80]{0,2,1:T(8,128)(2,1)S(1)}, bf16[1024,4,80]{0,2,1:T(8,128)(2,1)}, u32[]{:S(2)}) copy-start(bf16[1024,4,80]{0,2,1:T(8,128)(2,1)} %param.14) | copy-start | bytes 1966084
  32.4 11.2 %copy-start.4 = (bf16[1024,4,80]{0,2,1:T(8,128)(2,1)S(1)}, bf16[1024,4,80]{0,2,1:T(8,128)(2,1)}, u32[]{:S(2)}) copy-start(bf16[1024,4,80]{0,2,1:T(8,128)(2,1)} %param.13) | copy-start | bytes 1966084
  38.6 8.8 %collective-permute-start.3 = (bf16[40,1024]{1,0:T(8,128)(2,1)}, bf16[40,1024]{1,0:T(8,128)(2,1)}, u32[]{:S(2)}, u32[]{:S(2)}) collective-permute-start(bf16[40,1024]{1,0:T(8,128)(2,1)} %get-tuple-element.81), channel_id=1, source_target_pairs={{0,1},{1,2},{2,3},{3,0},{4,5},{5,6},{6,7},{7,4},{8,9},{9,10},{10,1... | collective-permute-start | bytes 245768 | tf_op jit(solution)/shard_map/ppermute | solution.py:18
  39.6 9.1 %collective-permute-start.5 = (bf16[40,1024]{1,0:T(8,128)(2,1)}, bf16[40,1024]{1,0:T(8,128)(2,1)}, u32[]{:S(2)}, u32[]{:S(2)}) collective-permute-start(bf16[40,1024]{1,0:T(8,128)(2,1)} %get-tuple-element.82), channel_id=1, source_target_pairs={{0,3},{1,0},{2,1},{3,2},{4,7},{5,4},{6,5},{7,6},{8,11},{9,8},{10,9... | collective-permute-start | bytes 245768 | tf_op jit(solution)/shard_map/ppermute | solution.py:18
  42.4 7.9 %collective-permute-start.4 = (bf16[40,1024]{1,0:T(8,128)(2,1)}, bf16[40,1024]{1,0:T(8,128)(2,1)}, u32[]{:S(2)}, u32[]{:S(2)}) collective-permute-start(bf16[40,1024]{1,0:T(8,128)(2,1)} %get-tuple-element.83), channel_id=1, source_target_pairs={{0,2},{1,3},{2,0},{3,1},{4,6},{5,7},{6,4},{7,5},{8,10},{9,11},{10,... | collective-permute-start | bytes 245768 | tf_op jit(solution)/shard_map/ppermute | solution.py:18
  47.4 14.4 %collective-permute-start = (bf16[40,1024]{1,0:T(8,128)(2,1)}, bf16[40,1024]{1,0:T(8,128)(2,1)S(1)}, u32[]{:S(2)}, u32[]{:S(2)}) collective-permute-start(bf16[40,1024]{1,0:T(8,128)(2,1)} %get-tuple-element.79), channel_id=1, source_target_pairs={{0,1},{1,2},{2,3},{3,0},{4,5},{5,6},{6,7},{7,4},{8,9},{9,10},{10,1... | collective-permute-start | bytes 245768 | tf_op jit(solution)/shard_map/ppermute | solution.py:18
  51.4 10.5 %copy-start.5 = (bf16[40,1024]{1,0:T(8,128)(2,1)S(1)}, bf16[40,1024]{1,0:T(8,128)(2,1)}, u32[]{:S(2)}) copy-start(bf16[40,1024]{1,0:T(8,128)(2,1)} %get-tuple-element.27) | copy-start | bytes 245764
  51.4 19.6 %collective-permute-start.11 = (bf16[40,1024]{1,0:T(8,128)(2,1)S(1)}, bf16[40,1024]{1,0:T(8,128)(2,1)S(1)}, u32[]{:S(2)}, u32[]{:S(2)}) collective-permute-start(bf16[40,1024]{1,0:T(8,128)(2,1)S(1)} %fusion.66), channel_id=1, source_target_pairs={{0,3},{1,0},{2,1},{3,2},{4,7},{5,4},{6,5},{7,6},{8,11},{9,8},{10,9... | collective-permute-start | bytes 245768 | tf_op jit(solution)/shard_map/ppermute | solution.py:30
  53.6 17.3 %collective-permute-start.10 = (bf16[40,1024]{1,0:T(8,128)(2,1)S(1)}, bf16[40,1024]{1,0:T(8,128)(2,1)S(1)}, u32[]{:S(2)}, u32[]{:S(2)}) collective-permute-start(bf16[40,1024]{1,0:T(8,128)(2,1)S(1)} %fusion.66), channel_id=1, source_target_pairs={{0,2},{1,3},{2,0},{3,1},{4,6},{5,7},{6,4},{7,5},{8,10},{9,11},{10,... | collective-permute-start | bytes 245768 | tf_op jit(solution)/shard_map/ppermute | solution.py:30
  53.8 17.2 %copy-start.1 = (f32[4,80,1024]{2,1,0:T(8,128)S(1)}, f32[4,80,1024]{2,1,0:T(8,128)}, u32[]{:S(2)}) copy-start(f32[4,80,1024]{2,1,0:T(8,128)} %get-tuple-element.90) | copy-start | bytes 3932164
  53.8 17.3 %copy-start.2 = (f32[4,80,1024]{2,1,0:T(8,128)S(1)}, f32[4,80,1024]{2,1,0:T(8,128)}, u32[]{:S(2)}) copy-start(f32[4,80,1024]{2,1,0:T(8,128)} %get-tuple-element.91) | copy-start | bytes 3932164
  61.3 9.7 %copy-start = (f32[4,80,1024]{2,1,0:T(8,128)S(1)}, f32[4,80,1024]{2,1,0:T(8,128)}, u32[]{:S(2)}) copy-start(f32[4,80,1024]{2,1,0:T(8,128)} %get-tuple-element.73) | copy-start | bytes 3932164
  61.3 7.2 %collective-permute-start.9 = (bf16[40,1024]{1,0:T(8,128)(2,1)S(1)}, bf16[40,1024]{1,0:T(8,128)(2,1)S(1)}, u32[]{:S(2)}, u32[]{:S(2)}) collective-permute-start(bf16[40,1024]{1,0:T(8,128)(2,1)S(1)} %fusion.66), channel_id=1, source_target_pairs={{0,1},{1,2},{2,3},{3,0},{4,5},{5,6},{6,7},{7,4},{8,9},{9,10},{10,1... | collective-permute-start | bytes 245768 | tf_op jit(solution)/shard_map/ppermute | solution.py:30
  62.9 19.8 %collective-permute-start.8 = (bf16[40,1024]{1,0:T(8,128)(2,1)S(1)}, bf16[40,1024]{1,0:T(8,128)(2,1)S(1)}, u32[]{:S(2)}, u32[]{:S(2)}) collective-permute-start(bf16[40,1024]{1,0:T(8,128)(2,1)S(1)} %add_convert_fusion), channel_id=1, source_target_pairs={{0,3},{1,0},{2,1},{3,2},{4,7},{5,4},{6,5},{7,6},{8,11},{9,8},{10,9... | collective-permute-start | bytes 245768 | tf_op jit(solution)/shard_map/ppermute | solution.py:30
  66.2 16.4 %collective-permute-start.7 = (bf16[40,1024]{1,0:T(8,128)(2,1)S(1)}, bf16[40,1024]{1,0:T(8,128)(2,1)S(1)}, u32[]{:S(2)}, u32[]{:S(2)}) collective-permute-start(bf16[40,1024]{1,0:T(8,128)(2,1)S(1)} %add_convert_fusion), channel_id=1, source_target_pairs={{0,2},{1,3},{2,0},{3,1},{4,6},{5,7},{6,4},{7,5},{8,10},{9,11},{10,... | collective-permute-start | bytes 245768 | tf_op jit(solution)/shard_map/ppermute | solution.py:30
  68.5 14.1 %collective-permute-start.6 = (bf16[40,1024]{1,0:T(8,128)(2,1)S(1)}, bf16[40,1024]{1,0:T(8,128)(2,1)S(1)}, u32[]{:S(2)}, u32[]{:S(2)}) collective-permute-start(bf16[40,1024]{1,0:T(8,128)(2,1)S(1)} %add_convert_fusion), channel_id=1, source_target_pairs={{0,1},{1,2},{2,3},{3,0},{4,5},{5,6},{6,7},{7,4},{8,9},{9,10},{10,1... | collective-permute-start | bytes 245768 | tf_op jit(solution)/shard_map/ppermute | solution.py:30
  71.4 17.5 %slice-start = ((s8[14680064]{0:T(1024)(128)(4,1)}), s8[2097152]{0:T(1024)(128)(4,1)S(1)}, s32[]{:S(2)}) async-start(s8[14680064]{0:T(1024)(128)(4,1)} %bitcast.114), calls=%async_computation.2 | async-start | bytes 4194304
  71.4 17.5 %slice-start.1 = ((s8[14680064]{0:T(1024)(128)(4,1)}), s8[4194304]{0:T(1024)(128)(4,1)S(1)}, s32[]{:S(2)}) async-start(s8[14680064]{0:T(1024)(128)(4,1)} %bitcast.114), calls=%async_computation.3 | async-start | bytes 8388608
  77.0 11.9 %slice-start.2 = ((s8[14680064]{0:T(1024)(128)(4,1)}), s8[4194304]{0:T(1024)(128)(4,1)S(1)}, s32[]{:S(2)}) async-start(s8[14680064]{0:T(1024)(128)(4,1)} %bitcast.114), calls=%async_computation.4 | async-start | bytes 8388608
  83.3 5.6 %slice-start.3 = ((s8[14680064]{0:T(1024)(128)(4,1)}), s8[4194304]{0:T(1024)(128)(4,1)S(1)}, s32[]{:S(2)}) async-start(s8[14680064]{0:T(1024)(128)(4,1)} %bitcast.114), calls=%async_computation.5 | async-start | bytes 8388608
  93.4 20.7 %all-to-all-start = ((bf16[8,32,1920]{2,1,0:T(8,128)(2,1)}), bf16[8,32,1920]{2,1,0:T(8,128)(2,1)S(1)}, u32[]{:S(2)}, u32[]{:S(2)}) async-start(bf16[8,32,1920]{2,1,0:T(8,128)(2,1)} %bitcast.34), calls=%async_computation | async-start | bytes 1966080 | tf_op jit(solution)/shard_map/all_to_all | solution.py:142
where the time goes:
time: 117 us; the launch traced here: 116 us
  matrix products  56.2 us (48%)
  starting transfers between devices  27.6 us (24%)
  blocking collectives  12.3 us (11%)
  other arithmetic  8.98 us (8%)
  local copies, waits for them, and re-layouts  6.86 us (6%)
  waiting for transfers between devices  2.95 us (3%)
    all_gather x1, blocking collectives, on_device(): packed = lax.all_gather(packed, GROUP, axis=0, tiled=True)  12.3 us
    dot_general x2, matrix products, on_device(): jnp.einsum('erf,edf->erd', part_up, w_up[cut], preferred_element_type=jnp...  11.1 us
    dot_general x2, matrix products, on_device(): jnp.einsum('erd,efd->erf', dy_rows[cut], w_down[cut], preferred_element_t...  10.9 us
    ppermute x6, starting transfers between devices, scatter_blocks(): lax.ppermute(piece, 'tp', [(i, (i + step) % parts) for i in range(parts)])  9.86 us
    ppermute x6, starting transfers between devices, gather_pieces(): return [block] + [lax.ppermute(block, 'tp', shift) for shift in shifts]  9.63 us
    dot_general x2, matrix products, on_device(): jnp.einsum('erf,edf->erd', part_gate, w_gate[cut], preferred_element_type...  7.96 us
    dot_general x1, matrix products, on_device(): jnp.einsum('erd,erf->edf', x_rows, d_gate, preferred_element_type=jnp.flo...  7.59 us
    dot_general x1, matrix products, on_device(): jnp.einsum('erf,erd->efd', hidden, scaled, preferred_element_type=jnp.flo...  7.57 us
  transfers between devices with their start and end apart: 14, of which 2 were waited for; matrix products, arithmetic and copies ran while one was open for 57% of the time, Pallas kernels for 0%

commit v1 on v0

--- a/solution.py
+++ b/solution.py
@@ -1,6 +1,9 @@
+import functools
 import jax
 import jax.numpy as jnp
 from jax import lax
+from jax.experimental import pallas as pl
+from jax.experimental.pallas import tpu as pltpu
 from jax.sharding import PartitionSpec as P
 
 LANES = 128
@@ -40,7 +43,7 @@
     return whole
 
 
-def on_device(tokens, cotangent, gates, expert_ids, saved_gate, saved_up, w_gate, w_up, w_down):
+def on_device_plain(tokens, cotangent, gates, expert_ids, saved_gate, saved_up, w_gate, w_up, w_down):
     groups = lax.axis_size(GROUP)
     parts = lax.axis_size("tp")
     rows, width = tokens.shape
@@ -159,6 +162,503 @@
     return (grad_tokens, grad_gates, grad_w_gate, grad_w_up, grad_w_down)
 
 
+MESH = pl.DeviceIdType.MESH
+HALVES = 2
+LAG = 2
+NT = (((1,), (1,)), ((), ()))
+
+
+def mm(a, b):
+    return jnp.dot(a, b, preferred_element_type=jnp.float32)
+
+
+def mm_dims(a, b, dims):
+    return lax.dot_general(a, b, dims, preferred_element_type=jnp.float32)
+
+
+def exchange_kernel(
+    cap,
+    gates_in, ids_in, cot, tok, act_gate, act_up, w_gate, w_up, w_down,
+    x_cols_out, scaled_out, hidden_out, d_gate_out, d_up_out, back_out,
+    small, dy_all, x_all, sm_all, wd, wg, wu, chosen, chosen_t, gate_rows,
+    x_cols, scaled, hidden_t, hidden, d_gate, d_up, back, to_gate, to_up,
+    own, from_end, pair, from_mid, total, dx_acc, back_acc, score_acc, score_cols,
+    w_sem, out_sem, dy_send, dy_recv, x_send, x_recv, sm_send, sm_recv,
+    end_send, end_recv, mid_send, mid_recv, tot_send, tot_recv,
+):
+    ex, ey, tp = lax.axis_index("ex"), lax.axis_index("ey"), lax.axis_index("tp")
+    n_ex, n_ey = lax.axis_size("ex"), lax.axis_size("ey")
+    n_tp = lax.axis_size("tp")
+    groups = n_ex * n_ey
+    group = ex * n_ey + ey
+    rows, width = cot.shape
+    top = gates_in.shape[0]
+    local, slots, ff = hidden.shape
+    tokens = groups * rows
+    chunks, _, piece = own.shape
+    per = chunks // local
+    first = group * local
+    is_end = (tp == 0) | (tp == n_tp - 1)
+    is_mid = (tp > 0) & (tp < n_tp - 1)
+    low = tp < n_tp // 2
+    near_mid = (ex, ey, jnp.where(low, 1, n_tp - 2))
+    near_end = (ex, ey, jnp.where(low, 0, n_tp - 1))
+    other_mid = (ex, ey, jnp.where(low, n_tp // 2, n_tp // 2 - 1))
+    partner = (ex, 1 - ey, tp)
+
+    def load(which, e):
+        src = (w_down, w_gate, w_up)[which]
+        dst = (wd, wg, wu)[which]
+        return pltpu.make_async_copy(src.at[e], dst.at[e], w_sem.at[which * local + e])
+
+    def save(which, e):
+        src = (x_cols, scaled, hidden_t, d_gate, d_up)[which]
+        dst = (x_cols_out, scaled_out, hidden_out, d_gate_out, d_up_out)[which]
+        return pltpu.make_async_copy(src.at[e], dst.at[e], out_sem.at[which * local + e])
+
+    for e in range(local):
+        load(0, e).start()
+
+    small[...] = jnp.full(small.shape, -1.0, small.dtype)
+    small[:top, :rows] = gates_in[...]
+    small[top : 2 * top, :rows] = ids_in[...].astype(jnp.float32).astype(jnp.bfloat16)
+
+    bar = pltpu.get_barrier_semaphore()
+    for s in range(1, n_ex):
+        pl.semaphore_signal(bar, inc=1, device_id=((ex + s) % n_ex, ey, tp), device_id_type=MESH)
+    pl.semaphore_signal(bar, inc=1, device_id=partner, device_id_type=MESH)
+
+    @pl.when(is_end)
+    def _():
+        pl.semaphore_signal(bar, inc=1, device_id=near_mid, device_id_type=MESH)
+
+    @pl.when(is_mid)
+    def _():
+        pl.semaphore_signal(bar, inc=1, device_id=near_end, device_id_type=MESH)
+        pl.semaphore_signal(bar, inc=1, device_id=other_mid, device_id_type=MESH)
+
+    with jax.named_scope("barrier"):
+        @pl.when(is_end)
+        def _():
+            pl.semaphore_wait(bar, n_ex + 1)
+
+        @pl.when(is_mid)
+        def _():
+            pl.semaphore_wait(bar, n_ex + 2)
+
+    def remote(src, dst, send, recv, to):
+        return pltpu.make_async_remote_copy(
+            src_ref=src, dst_ref=dst, send_sem=send, recv_sem=recv,
+            device_id=to, device_id_type=MESH,
+        )
+
+    def spread(src, dest, send, recv):
+        for s in range(1, n_ex):
+            to = ((ex + s) % n_ex, ey, tp)
+            remote(src, dest.at[group], send.at[s - 1], recv.at[group], to).start()
+        remote(src, dest.at[group], send.at[n_ex - 1], recv.at[group], partner).start()
+
+    def relay(dest, send, recv):
+        for s in range(1, n_ex):
+            origin = ((ex - s + n_ex) % n_ex) * n_ey + ey
+            blk = dest.at[origin]
+            copy = remote(blk, blk, send.at[n_ex - 1 + s], recv.at[origin], partner)
+            copy.wait_recv()
+            copy.start()
+
+    def rest(dest, send, recv):
+        for c in range(n_ex):
+            blk = dest.at[c * n_ey + 1 - ey]
+            remote(blk, blk, send.at[0], recv.at[c * n_ey + 1 - ey], partner).wait_recv()
+
+    def drain(src, dest, send, recv):
+        for i in range(2 * n_ex - 1):
+            remote(src, dest.at[group], send.at[i], recv.at[group], partner).wait_send()
+
+    spread(small, sm_all, sm_send, sm_recv)
+    spread(cot, dy_all, dy_send, dy_recv)
+
+    def activations(e, carry):
+        a = act_gate[e].astype(jnp.float32)
+        u = act_up[e].astype(jnp.float32)
+        q = 1.0 / (1.0 + jnp.exp(-a))
+        silu = a * q
+        hid = silu * u
+        hidden[e] = hid.astype(jnp.bfloat16)
+        hidden_t[e] = hid.T.astype(jnp.bfloat16)
+        to_gate[e] = u * q * (1.0 + a * (1.0 - q))
+        to_up[e] = silu
+        save(2, e).start()
+        return carry
+
+    with jax.named_scope("acts"):
+        sm_all[group] = small[...]
+        dy_all[group] = cot[...]
+        x_all[group] = tok[...]
+        lax.fori_loop(0, local, activations, 0)
+
+    with jax.named_scope("small"):
+        relay(sm_all, sm_send, sm_recv)
+        rest(sm_all, sm_send, sm_recv)
+
+    with jax.named_scope("routing"):
+        def lanes_of(part):
+            tiles = []
+            for base in range(0, tokens, LANES):
+                acc = None
+                for g in range(base // rows, min(groups, (base + LANES) // rows)):
+                    block = sm_all[g].astype(jnp.float32)[part * top : (part + 1) * top]
+                    at = g * rows - base
+                    moved = pltpu.roll(block, at, axis=1) if at else block
+                    lane = lax.broadcasted_iota(jnp.int32, (top, LANES), 1)
+                    moved = jnp.where((lane >= at) & (lane < at + rows), moved, 0.0)
+                    acc = moved if acc is None else acc + moved
+                tiles.append(acc)
+            return jnp.concatenate(tiles, axis=1)
+
+        gates = lanes_of(0)
+        ids = lanes_of(1)
+        start = lax.broadcasted_iota(jnp.int32, (groups, rows, tokens), 0).reshape(tokens, tokens)
+        at_row = lax.broadcasted_iota(jnp.int32, (tokens, tokens), 0)
+        at_col = lax.broadcasted_iota(jnp.int32, (tokens, tokens), 1)
+        after = (at_row < at_col) & (at_col < (start + 1) * rows)
+        after = jnp.where(after, 1.0, 0.0).astype(jnp.bfloat16)
+        row = lax.broadcasted_iota(jnp.int32, (top, tokens), 0)
+        names = jnp.zeros((top, tokens), jnp.float32)
+        named, gate_of = [], []
+        for e in range(local):
+            hit = ids == (first + e).astype(jnp.float32)
+            named.append(jnp.sum(jnp.where(hit, 1.0, 0.0), axis=0, keepdims=True))
+            gate_of.append(jnp.sum(jnp.where(hit, gates, 0.0), axis=0, keepdims=True))
+            names = names + jnp.where(row == e, named[e], 0.0)
+        position = mm(names.astype(jnp.bfloat16), after)
+        lane = lax.broadcasted_iota(jnp.int32, (1, tokens), 1)
+        base = jnp.zeros((1, tokens), jnp.int32)
+        for g in range(1, groups):
+            base = base + jnp.where(lane >= g * rows, cap, 0)
+        base = base.astype(jnp.float32)
+        slot = lax.broadcasted_iota(jnp.int32, (LANES, tokens), 0).astype(jnp.float32)
+        for e in range(local):
+            row_of = jnp.where(named[e] > 0.0, base + position[e : e + 1], -1.0)
+            pick = jnp.where(slot == row_of, 1.0, 0.0)
+            chosen[e] = pick[:slots].astype(jnp.bfloat16)
+            chosen_t[e] = pick.T.astype(jnp.bfloat16)
+            g_col = jnp.sum(pick[:slots] * gate_of[e], axis=1, keepdims=True)
+            gate_rows[e] = jnp.broadcast_to(g_col, (slots, LANES))
+
+    with jax.named_scope("dyrecv"):
+        relay(dy_all, dy_send, dy_recv)
+        for e in range(local):
+            load(1, e).start()
+            load(2, e).start()
+        spread(tok, x_all, x_send, x_recv)
+        rest(dy_all, dy_send, dy_recv)
+
+    def to_mid(c):
+        return remote(own.at[c], from_end.at[c], end_send.at[c], end_recv.at[c], near_mid)
+
+    def to_pair(c):
+        return remote(pair.at[c], from_mid.at[c], mid_send.at[c], mid_recv.at[c], other_mid)
+
+    def to_end(c):
+        return remote(total.at[c], total.at[c], tot_send.at[c], tot_recv.at[c], near_end)
+
+    def first_pass(e, carry):
+        dy = mm(chosen[e], dy_all[...].reshape(tokens, width)).astype(jnp.bfloat16)
+        scaled[e] = (gate_rows[e][:, :1] * dy.astype(jnp.float32)).astype(jnp.bfloat16)
+        load(0, e).wait()
+        for h in range(per):
+            raw = mm_dims(dy, wd[e, h * piece : (h + 1) * piece, :], NT)
+            own[e * per + h] = raw.astype(jnp.bfloat16)
+
+            @pl.when(is_end)
+            def _():
+                to_mid(e * per + h).start()
+
+        save(1, e).start()
+        return carry
+
+    with jax.named_scope("first"):
+        lax.fori_loop(0, local, first_pass, 0)
+
+    def join(c):
+        to_mid(c).wait_recv()
+        pair[c] = (own[c].astype(jnp.float32) + from_end[c].astype(jnp.float32)).astype(jnp.bfloat16)
+        to_pair(c).start()
+
+    def arrive(c):
+        @pl.when(is_mid & (c + LAG < chunks))
+        def _():
+            join(c + LAG)
+
+        @pl.when(is_mid)
+        def _():
+            to_pair(c).wait_recv()
+            both = pair[c].astype(jnp.float32) + from_mid[c].astype(jnp.float32)
+            total[c] = both.astype(jnp.bfloat16)
+            to_end(c).start()
+
+        @pl.when(is_end)
+        def _():
+            to_end(c).wait_recv()
+
+    with jax.named_scope("lead"):
+        @pl.when(is_mid)
+        def _():
+            for c in range(LAG):
+                join(c)
+
+        back_acc[...] = jnp.zeros_like(back_acc)
+        score_acc[...] = jnp.zeros_like(score_acc)
+
+    def place(e, carry):
+        rows_of = mm(chosen[e], x_all[...].reshape(tokens, width))
+        x_cols[e] = rows_of.T.astype(jnp.bfloat16)
+        save(0, e).start()
+        return carry
+
+    def second_pass(e, carry):
+        for h in range(per):
+            c = e * per + h
+            with jax.named_scope("arrive"):
+                arrive(c)
+
+            with jax.named_scope("dx"):
+                span = slice(h * piece, (h + 1) * piece)
+                raw = total[c].astype(jnp.float32)
+                dh = gate_rows[e][:, :1] * raw
+                dg = (dh * to_gate[e, :, span]).astype(jnp.bfloat16)
+                du = (dh * to_up[e, :, span]).astype(jnp.bfloat16)
+                d_gate[e, :, span] = dg
+                d_up[e, :, span] = du
+                part = jnp.sum(raw * hidden[e, :, span].astype(jnp.float32), axis=1, keepdims=True)
+                if h == 0:
+                    score_cols[...] = jnp.broadcast_to(part, score_cols.shape)
+
+                    @pl.when(e == 0)
+                    def _():
+                        for i in range(local):
+                            load(1, i).wait()
+                            load(2, i).wait()
+                else:
+                    score_cols[...] += part
+                dx = mm_dims(dg, wg[e, :, span], NT) + mm_dims(du, wu[e, :, span], NT)
+                if h == 0:
+                    dx_acc[...] = dx
+                else:
+                    dx_acc[...] += dx
+        with jax.named_scope("back"):
+            save(3, e).start()
+            save(4, e).start()
+            pick = chosen_t[e][:, :slots]
+            back_acc[...] += mm(pick, dx_acc[...].astype(jnp.bfloat16))
+            at = lax.broadcasted_iota(jnp.int32, (slots, LANES), 1)
+            score = jnp.where(at == e, score_cols[...], 0.0).astype(jnp.bfloat16)
+            score_acc[...] += mm(pick, score)
+
+        @pl.when(e == 0)
+        def _():
+            with jax.named_scope("xrelay"):
+                relay(x_all, x_send, x_recv)
+
+        @pl.when(e == 1)
+        def _():
+            with jax.named_scope("xplace"):
+                rest(x_all, x_send, x_recv)
+                lax.fori_loop(0, local, place, 0)
+
+        return carry
+
+    lax.fori_loop(0, local, second_pass, 0)
+    with jax.named_scope("finish"):
+        back[:, :, :width] = back_acc[...].astype(jnp.bfloat16).reshape(groups, rows, width)
+        back[:, :, width:] = score_acc[...].astype(jnp.bfloat16).reshape(groups, rows, LANES)
+        last = pltpu.make_async_copy(back, back_out, out_sem.at[5 * local])
+        last.start()
+        drain(small, sm_all, sm_send, sm_recv)
+        drain(cot, dy_all, dy_send, dy_recv)
+        drain(tok, x_all, x_send, x_recv)
+
+        @pl.when(is_end)
+        def _():
+            for c in range(chunks):
+                to_mid(c).wait_send()
+
+        @pl.when(is_mid)
+        def _():
+            for c in range(chunks):
+                to_pair(c).wait_send()
+                to_end(c).wait_send()
+
+        for which in range(5):
+            for e in range(local):
+                save(which, e).wait()
+        last.wait()
+
+
+def exchange(cap, groups, gates, ids, cot, tok, act_gate, act_up, w_gate, w_up, w_down):
+    rows, width = cot.shape
+    local, slots, ff = act_gate.shape
+    tokens = groups * rows
+    chunks = local * HALVES
+    piece = ff // HALVES
+    n_ex, n_ey = lax.axis_size("ex"), lax.axis_size("ey")
+    bf, f32 = jnp.bfloat16, jnp.float32
+    sends = 2 * n_ex - 1
+    dma = pltpu.SemaphoreType.DMA
+    vmem = pl.BlockSpec(memory_space=pltpu.VMEM)
+    hbm = pl.BlockSpec(memory_space=pltpu.HBM)
+    buf = pltpu.VMEM((chunks, slots, piece), bf)
+    outs = (
+        (local, width, slots), (local, slots, width), (local, ff, slots),
+        (local, slots, ff), (local, slots, ff), (groups, rows, width + LANES),
+    )
+    return pl.pallas_call(
+        functools.partial(exchange_kernel, cap),
+        out_shape=tuple(jax.ShapeDtypeStruct(shape, bf) for shape in outs),
+        in_specs=[vmem] * 6 + [hbm] * 3,
+        out_specs=(hbm,) * 6,
+        scratch_shapes=[
+            pltpu.VMEM((2 * gates.shape[0], LANES), bf),
+            pltpu.VMEM((groups, rows, width), bf),
+            pltpu.VMEM((groups, rows, width), bf),
+            pltpu.VMEM((groups, 2 * gates.shape[0], LANES), bf),
+            pltpu.VMEM((local, ff, width), bf),
+            pltpu.VMEM((local, width, ff), bf),
+            pltpu.VMEM((local, width, ff), bf),
+            pltpu.VMEM((local, slots, tokens), bf),
+            pltpu.VMEM((local, tokens, LANES), bf),
+            pltpu.VMEM((local, slots, LANES), f32),
+            pltpu.VMEM((local, width, slots), bf),
+            pltpu.VMEM((local, slots, width), bf),
+            pltpu.VMEM((local, ff, slots), bf),
+            pltpu.VMEM((local, slots, ff), bf),
+            pltpu.VMEM((local, slots, ff), bf),
+            pltpu.VMEM((local, slots, ff), bf),
+            pltpu.VMEM((groups, rows, width + LANES), bf),
+            pltpu.VMEM((local, slots, ff), f32),
+            pltpu.VMEM((local, slots, ff), f32),
+            buf, buf, buf, buf, buf,
+            pltpu.VMEM((slots, width), f32),
+            pltpu.VMEM((tokens, width), f32),
+            pltpu.VMEM((tokens, LANES), f32),
+            pltpu.VMEM((slots, LANES), f32),
+            dma((3 * local,)), dma((5 * local + 1,)),
+            dma((sends,)), dma((groups,)),
+            dma((sends,)), dma((groups,)),
+            dma((sends,)), dma((groups,)),
+            dma((chunks,)), dma((chunks,)),
+            dma((chunks,)), dma((chunks,)),
+            dma((chunks,)), dma((chunks,)),
+        ],
+        compiler_params=pltpu.CompilerParams(
+            collective_id=0, has_side_effects=True, vmem_limit_bytes=63 << 20
+        ),
+        name="exchange",
+    )(gates, ids, cot, tok, act_gate, act_up, w_gate, w_up, w_down)
+
+
+def weights_kernel(
+    x_cols_in, scaled_in, hidden_in, d_gate_in, d_up_in,
+    down_out, gate_out, up_out,
+    x_cols, scaled, hidden, d_gate, d_up, down, gate, up, in_sem, out_sem,
+):
+    local, width, slots = x_cols.shape
+    ff = hidden.shape[1]
+    tile = 256
+    steps = width // tile
+
+    def load(which, e):
+        src = (hidden_in, scaled_in, x_cols_in, d_gate_in, d_up_in)[which]
+        dst = (hidden, scaled, x_cols, d_gate, d_up)[which]
+        return pltpu.make_async_copy(src.at[e], dst.at[e], in_sem.at[which, e])
+
+    def save(which, e, j):
+        src = (down, gate, up)[which]
+        dst = (down_out, gate_out, up_out)[which]
+        at = pl.ds(pl.multiple_of(j * tile, tile), tile)
+        index = (e, slice(None), at) if which == 0 else (e, at)
+        return pltpu.make_async_copy(src.at[index], dst.at[index], out_sem.at[which, e * steps + j])
+
+    for e in range(local):
+        for which in range(5):
+            load(which, e).start()
+
+    def expert(e, carry):
+        for which in range(5):
+            load(which, e).wait()
+
+        def step(j, carry):
+            at = pl.ds(pl.multiple_of(j * tile, tile), tile)
+            x_t = x_cols[e, at, :]
+            gate[e, at, :] = mm(x_t, d_gate[e]).astype(jnp.bfloat16)
+            save(1, e, j).start()
+            up[e, at, :] = mm(x_t, d_up[e]).astype(jnp.bfloat16)
+            save(2, e, j).start()
+            down[e, :, at] = mm(hidden[e], scaled[e, :, at]).astype(jnp.bfloat16)
+            save(0, e, j).start()
+            return carry
+
+        return lax.fori_loop(0, steps, step, carry)
+
+    lax.fori_loop(0, local, expert, 0)
+
+    def finish(e, carry):
+        for which in range(3):
+            for j in range(steps):
+                save(which, e, j).wait()
+        return carry
+
+    lax.fori_loop(0, local, finish, 0)
+
+
+def weight_grads(x_cols, scaled, hidden, d_gate, d_up):
+    local, width, slots = x_cols.shape
+    ff = hidden.shape[1]
+    bf = jnp.bfloat16
+    hbm = pl.BlockSpec(memory_space=pltpu.HBM)
+    outs = ((local, ff, width), (local, width, ff), (local, width, ff))
+    ins = [pltpu.VMEM(part.shape, bf) for part in (x_cols, scaled, hidden, d_gate, d_up)]
+    dma = pltpu.SemaphoreType.DMA
+    return pl.pallas_call(
+        weights_kernel,
+        out_shape=tuple(jax.ShapeDtypeStruct(shape, bf) for shape in outs),
+        in_specs=[hbm] * 5,
+        out_specs=(hbm,) * 3,
+        scratch_shapes=ins
+        + [pltpu.VMEM(shape, bf) for shape in outs]
+        + [dma((5, local)), dma((3, local * (width // 256)))],
+        compiler_params=pltpu.CompilerParams(vmem_limit_bytes=60 << 20),
+        cost_estimate=pl.CostEstimate(
+            flops=6 * local * slots * ff * width,
+            bytes_accessed=6 * local * ff * width,
+            transcendentals=0,
+        ),
+        name="weight_grads",
+    )(x_cols, scaled, hidden, d_gate, d_up)
+
+
+def on_device(tokens, cotangent, gates, expert_ids, saved_gate, saved_up, w_gate, w_up, w_down):
+    groups = lax.axis_size(GROUP)
+    rows, width = tokens.shape
+    local, slots = saved_gate.shape[1:]
+    act_gate = saved_gate.transpose(1, 2, 0)
+    act_up = saved_up.transpose(1, 2, 0)
+    x_cols, scaled, hidden, d_gate, d_up, back = exchange(
+        slots // groups, groups, gates.T, expert_ids.T, cotangent, tokens,
+        act_gate, act_up, w_gate, w_up, w_down,
+    )
+    back = lax.all_to_all(back, GROUP, split_axis=0, concat_axis=0, tiled=True)
+    grad_w_down, grad_w_gate, grad_w_up = weight_grads(x_cols, scaled, hidden, d_gate, d_up)
+    grad_tokens = jnp.sum(back[:, :, :width].astype(jnp.float32), axis=0).astype(jnp.bfloat16)
+    table = back[:, :, width : width + local].transpose(1, 0, 2).reshape(rows, groups * local)
+    picks = expert_ids[:, :, None] == jnp.arange(groups * local, dtype=jnp.int32)[None, None, :]
+    grad_gates = jnp.sum(
+        jnp.where(picks, table.astype(jnp.float32)[:, None, :], 0.0), axis=2
+    ).astype(jnp.bfloat16)
+    return (grad_tokens, grad_gates, grad_w_gate, grad_w_up, grad_w_down)
+
+
 def solution(mesh):
     by_group = P(GROUP, "tp")
     small = P(GROUP, None)
@@ -167,6 +667,7 @@
     down = P(GROUP, None, "tp")
     in_specs = (by_group, by_group, small, small, saved, saved, wide, wide, down)
     out_specs = (by_group, small, wide, wide, down)
+    fast = mesh.shape["tp"] == 4 and mesh.shape["ey"] == 2
     return jax.shard_map(
-        on_device, mesh=mesh, in_specs=in_specs, out_specs=out_specs, check_vma=False
+        on_device if fast else on_device_plain, mesh=mesh, in_specs=in_specs, out_specs=out_specs, check_vma=False
     )

time: 117 us -> 70.8 us (0.61)
  Pallas kernels: 0 us -> 63.8 us
  matrix products: 56.2 us -> 0 us
  starting transfers between devices: 27.6 us -> 3.57 us
  blocking collectives: 12.3 us -> 0 us
  other arithmetic: 8.98 us -> 0.98 us
  local copies, waits for them, and re-layouts: 6.86 us -> 1.61 us
  waiting for transfers between devices: 2.95 us -> 0.01 us
    pallas_call x0 -> x2, Pallas kernels: none -> 63.8 us  [the longest x1 45.4 us: exchange(): pl.pallas_call(functools.partial(exchange_kernel, cap), out_shape=tuple((...]
    dot_general x14 -> x0, matrix products: 56.2 us -> none  [the longest x2 11.1 us: on_device(): jnp.einsum('erf,edf->erd', part_up, w_up[cut], preferred_element_type=jnp...]
    ppermute x12 -> x0, starting transfers between devices: 19.5 us -> none  [the longest x6 9.86 us: scatter_blocks(): lax.ppermute(piece, 'tp', [(i, (i + step) % parts) for i in range(parts)])]
    all_gather x1 -> x0, blocking collectives: 12.3 us -> none  [on_device(): packed = lax.all_gather(packed, GROUP, axis=0, tiled=True)]
    convert_element_type x8 -> x0, other arithmetic: 4.99 us -> none  [the longest x2 1.98 us: block_sum(): sum((term.astype(jnp.float32) for term in terms)).astype(jnp.bfloat16)]
    all_to_all x1 -> x0, starting transfers between devices: 4.23 us -> none  [on_device(): lax.all_to_all(jnp.broadcast_to(tokens[None], (groups, rows, width)), GRO...]
    ppermute x12 -> x0, waiting for transfers between devices: 2.94 us -> none  [the longest x6 1.65 us: scatter_blocks(): lax.ppermute(piece, 'tp', [(i, (i + step) % parts) for i in range(parts)])]
    div x1 -> x0, other arithmetic: 1.52 us -> none  [on_device(): sigm = jax.nn.sigmoid(act_gate)]
  transfers between devices with their start and end apart: 14 -> 1, of which waited for: 2 -> 0; matrix products, arithmetic and copies ran while one was open for 57% -> 1% of each run, Pallas kernels for 0% -> 26%
where the time goes in v1:
time: 70.8 us; the launch traced here: 70.6 us
  Pallas kernels  63.8 us (90%)
  starting transfers between devices  3.57 us (5%)
  local copies, waits for them, and re-layouts  1.61 us (2%)
  other arithmetic  0.98 us (1%)
    pallas_call x1, Pallas kernels, exchange(): pl.pallas_call(functools.partial(exchange_kernel, cap), out_shape=tuple((...  45.4 us
    pallas_call x1, Pallas kernels, weight_grads(): pl.pallas_call(weights_kernel, out_shape=tuple((jax.ShapeDtypeStruct(shap...  18.4 us
    all_to_all x1, starting transfers between devices, on_device(): back = lax.all_to_all(back, GROUP, split_axis=0, concat_axis=0, tiled=True)  3.57 us
    unnamed x2, local copies, waits for them, and re-layouts  1.43 us
  transfers between devices with their start and end apart: 1, of which 0 were waited for; matrix products, arithmetic and copies ran while one was open for 1% of the time, Pallas kernels for 26%

profile of v1, /device:TPU:0, one launch (start us, length us, event | category | flops | bytes accessed | tf_op | source)
XLA Modules:
  0.0 70.6 jit_solution(18426534692377429499)
XLA Ops:
  0.6 45.4 %exchange.1 = (bf16[4,1792,80]{2,1,0:T(8,128)(2,1)}, bf16[4,80,1792]{2,1,0:T(8,128)(2,1)}, bf16[4,1024,80]{2,1,0:T(8,128)(2,1)}, bf16[4,80,1024]{2,1,0:T(8,128)(...) custom-call(bf16[8,32]{1,0:T(8,128)(2,1)} %bitcast.11, s32[8,32]{1,0:T(8,128)} %bitcast.10, ...), custom_call_target="tpu_custom_call" | custom-call | tf_op jit(solution)/shard_map/exchange/pallas_call | solution.py:516
  46.0 3.6 %all-to-all-start = ((bf16[8,32,1920]{2,1,0:T(8,128)(2,1)}), bf16[8,32,1920]{2,1,0:T(8,128)(2,1)S(1)}, u32[]{:S(2)}, u32[]{:S(2)}) async-start(bf16[8,32,1920]{2,1,0:T(8,128)(2,1)} %get-tuple-element.14), calls=%async_computation | async-start | bytes 1966080 | tf_op jit(solution)/shard_map/all_to_all | solution.py:651
  49.6 0.8 %copy.18 = s32[32,8]{1,0:T(8,128)S(1)} copy(s32[32,8]{0,1:T(8,128)} %param.12) | data formatting | bytes 2048 | tf_op args[3]
  50.4 18.4 %weight_grads.1 = (bf16[4,1024,1792]{2,1,0:T(8,128)(2,1)}, bf16[4,1792,1024]{2,1,0:T(8,128)(2,1)}, bf16[4,1792,1024]{2,1,0:T(8,128)(2,1)}) custom-call(bf16[4,1792,80]{2,1,0:T(8,128)(2,1)} %get-tuple-element.15.x_cols_in, bf16[4,80,1792]{2,1,0:T(8,128)(2,1)} %get-tuple-element.16.scaled_in, bf16[4,1024,80]{2,1,0:T(8,128)(2,1)} %get-tuple-element.17.hidden_in, ...), custom_call_target="tpu_custom_call" | custom-call | flops 3523215360 | bytes 44040192 | tf_op jit(solution)/shard_map/weight_grads/pallas_call | solution.py:623
  68.8 0.0 all-to-all-done
  68.8 0.1 copy.19
  68.9 0.1 copy.20
  69.0 0.2 select_reduce_fusion
  69.2 0.7 copy.21
  69.9 0.8 %slice_reduce_fusion = bf16[32,1792]{1,0:T(8,128)(2,1)} fusion(bf16[8,32,1920]{2,1,0:T(8,128)(2,1)S(1)} %all-to-all-done), kind=kLoop, calls=%fused_computation | loop fusion | flops 401408 | bytes 1032192 | tf_op jit(solution)/shard_map/reduce_sum | solution.py:653
  (1 shorter events, 0.0 us)
Async XLA Ops:
  46.0 22.8 %all-to-all-start = ((bf16[8,32,1920]{2,1,0:T(8,128)(2,1)}), bf16[8,32,1920]{2,1,0:T(8,128)(2,1)S(1)}, u32[]{:S(2)}, u32[]{:S(2)}) async-start(bf16[8,32,1920]{2,1,0:T(8,128)(2,1)} %get-tuple-element.14), calls=%async_computation | async-start | bytes 1966080 | tf_op jit(solution)/shard_map/all_to_all | solution.py:651

commit v2 on v1

--- a/solution.py
+++ b/solution.py
@@ -163,8 +163,9 @@
 
 
 MESH = pl.DeviceIdType.MESH
-HALVES = 2
+SPLIT = 2
 LAG = 2
+STEPS = 2
 NT = (((1,), (1,)), ((), ()))
 
 
@@ -178,13 +179,14 @@
 
 def exchange_kernel(
     cap,
-    gates_in, ids_in, cot, tok, act_gate, act_up, w_gate, w_up, w_down,
+    gates_hbm, ids_hbm, cot_hbm, tok_hbm, gate_in, up_in, w_gate, w_up, w_down,
     x_cols_out, scaled_out, hidden_out, d_gate_out, d_up_out, back_out,
     small, dy_all, x_all, sm_all, wd, wg, wu, chosen, chosen_t, gate_rows,
     x_cols, scaled, hidden_t, hidden, d_gate, d_up, back, to_gate, to_up,
-    own, from_end, pair, from_mid, total, dx_acc, back_acc, score_acc, score_cols,
-    w_sem, out_sem, dy_send, dy_recv, x_send, x_recv, sm_send, sm_recv,
-    end_send, end_recv, mid_send, mid_recv, tot_send, tot_recv,
+    own, from_end, pair, from_mid, total, dx_acc, dx_rows, score_rows, score_cols,
+    dy_rows, act_gate, act_up, gates_in, ids_in, cot, tok,
+    w_sem, act_sem, head_sem, out_sem, dy_send, dy_recv, x_send, x_recv, sm_send, sm_recv,
+    end_send, end_recv, mid_send, mid_recv,
 ):
     ex, ey, tp = lax.axis_index("ex"), lax.axis_index("ey"), lax.axis_index("tp")
     n_ex, n_ey = lax.axis_size("ex"), lax.axis_size("ey")
@@ -209,20 +211,34 @@
     def load(which, e):
         src = (w_down, w_gate, w_up)[which]
         dst = (wd, wg, wu)[which]
-        return pltpu.make_async_copy(src.at[e], dst.at[e], w_sem.at[which * local + e])
+        return pltpu.make_async_copy(src.at[e], dst.at[e], w_sem.at[which])
+
+    def loaded(which):
+        src = (w_down, w_gate, w_up)[which]
+        dst = (wd, wg, wu)[which]
+        pltpu.make_async_copy(src, dst, w_sem.at[which]).wait()
+
+    saves = (
+        (x_cols, x_cols_out), (scaled, scaled_out), (hidden_t, hidden_out),
+        (d_gate, d_gate_out), (d_up, d_up_out),
+    )
 
     def save(which, e):
-        src = (x_cols, scaled, hidden_t, d_gate, d_up)[which]
-        dst = (x_cols_out, scaled_out, hidden_out, d_gate_out, d_up_out)[which]
-        return pltpu.make_async_copy(src.at[e], dst.at[e], out_sem.at[which * local + e])
-
-    for e in range(local):
-        load(0, e).start()
-
-    small[...] = jnp.full(small.shape, -1.0, small.dtype)
-    small[:top, :rows] = gates_in[...]
-    small[top : 2 * top, :rows] = ids_in[...].astype(jnp.float32).astype(jnp.bfloat16)
-
+        src, dst = saves[which]
+        return pltpu.make_async_copy(src.at[e], dst.at[e], out_sem.at[which])
+
+    heads = [
+        pltpu.make_async_copy(src, dst, head_sem.at[i])
+        for i, (src, dst) in enumerate(
+            ((gates_hbm, gates_in), (ids_hbm, ids_in), (cot_hbm, cot), (tok_hbm, tok))
+        )
+    ]
+    for copy in heads:
+        copy.start()
+    in_acts = (
+        pltpu.make_async_copy(gate_in, act_gate, act_sem.at[0]),
+        pltpu.make_async_copy(up_in, act_up, act_sem.at[1]),
+    )
     bar = pltpu.get_barrier_semaphore()
     for s in range(1, n_ex):
         pl.semaphore_signal(bar, inc=1, device_id=((ex + s) % n_ex, ey, tp), device_id_type=MESH)
@@ -236,6 +252,19 @@
     def _():
         pl.semaphore_signal(bar, inc=1, device_id=near_end, device_id_type=MESH)
         pl.semaphore_signal(bar, inc=1, device_id=other_mid, device_id_type=MESH)
+
+    for copy in in_acts:
+        copy.start()
+    for e in range(local):
+        load(0, e).start()
+    with jax.named_scope("heads"):
+        for copy in heads:
+            copy.wait()
+        small[...] = jnp.full(small.shape, -1.0, small.dtype)
+        small[:top, :rows] = gates_in[...]
+        small[top : 2 * top, :rows] = ids_in[...].astype(jnp.float32).astype(jnp.bfloat16)
+        dy_all[group] = cot[...]
+        x_all[group] = tok[...]
 
     with jax.named_scope("barrier"):
         @pl.when(is_end)
@@ -253,27 +282,25 @@
         )
 
     def spread(src, dest, send, recv):
+        mine = dest.at[group]
         for s in range(1, n_ex):
             to = ((ex + s) % n_ex, ey, tp)
-            remote(src, dest.at[group], send.at[s - 1], recv.at[group], to).start()
-        remote(src, dest.at[group], send.at[n_ex - 1], recv.at[group], partner).start()
+            remote(src, mine, send.at[0], recv.at[s - 1], to).start()
+        remote(src, mine, send.at[0], recv.at[n_ex - 1], partner).start()
 
     def relay(dest, send, recv):
         for s in range(1, n_ex):
-            origin = ((ex - s + n_ex) % n_ex) * n_ey + ey
-            blk = dest.at[origin]
-            copy = remote(blk, blk, send.at[n_ex - 1 + s], recv.at[origin], partner)
-            copy.wait_recv()
-            copy.start()
+            blk = dest.at[((ex - s + n_ex) % n_ex) * n_ey + ey]
+            remote(blk, blk, send.at[0], recv.at[s - 1], partner).wait_recv()
+            remote(blk, blk, send.at[0], recv.at[n_ex - 1], partner).start()
 
     def rest(dest, send, recv):
-        for c in range(n_ex):
-            blk = dest.at[c * n_ey + 1 - ey]
-            remote(blk, blk, send.at[0], recv.at[c * n_ey + 1 - ey], partner).wait_recv()
-
-    def drain(src, dest, send, recv):
-        for i in range(2 * n_ex - 1):
-            remote(src, dest.at[group], send.at[i], recv.at[group], partner).wait_send()
+        blks = dest.at[pl.ds(0, n_ex)]
+        remote(blks, blks, send.at[0], recv.at[n_ex - 1], partner).wait_recv()
+
+    def drain(dest, send, recv):
+        blks = dest.at[pl.ds(0, 2 * n_ex - 1)]
+        remote(blks, blks, send.at[0], recv.at[0], partner).wait_send()
 
     spread(small, sm_all, sm_send, sm_recv)
     spread(cot, dy_all, dy_send, dy_recv)
@@ -291,15 +318,14 @@
         save(2, e).start()
         return carry
 
-    with jax.named_scope("acts"):
-        sm_all[group] = small[...]
-        dy_all[group] = cot[...]
-        x_all[group] = tok[...]
-        lax.fori_loop(0, local, activations, 0)
+    sm_all[group] = small[...]
 
     with jax.named_scope("small"):
         relay(sm_all, sm_send, sm_recv)
         rest(sm_all, sm_send, sm_recv)
+        for e in range(local):
+            load(1, e).start()
+            load(2, e).start()
 
     with jax.named_scope("routing"):
         def lanes_of(part):
@@ -341,50 +367,69 @@
         for e in range(local):
             row_of = jnp.where(named[e] > 0.0, base + position[e : e + 1], -1.0)
             pick = jnp.where(slot == row_of, 1.0, 0.0)
-            chosen[e] = pick[:slots].astype(jnp.bfloat16)
-            chosen_t[e] = pick.T.astype(jnp.bfloat16)
+            chosen[e * slots : (e + 1) * slots] = pick[:slots].astype(jnp.bfloat16)
             g_col = jnp.sum(pick[:slots] * gate_of[e], axis=1, keepdims=True)
             gate_rows[e] = jnp.broadcast_to(g_col, (slots, LANES))
+        chosen_t[...] = chosen[...].astype(jnp.float32).T.astype(jnp.bfloat16)
+
+    with jax.named_scope("acts"):
+        for copy in in_acts:
+            copy.wait()
+        lax.fori_loop(0, local, activations, 0)
 
     with jax.named_scope("dyrecv"):
         relay(dy_all, dy_send, dy_recv)
-        for e in range(local):
-            load(1, e).start()
-            load(2, e).start()
         spread(tok, x_all, x_send, x_recv)
         rest(dy_all, dy_send, dy_recv)
 
     def to_mid(c):
-        return remote(own.at[c], from_end.at[c], end_send.at[c], end_recv.at[c], near_mid)
+        return remote(own.at[c], from_end.at[c], end_send.at[0], end_recv.at[c], near_mid)
 
     def to_pair(c):
-        return remote(pair.at[c], from_mid.at[c], mid_send.at[c], mid_recv.at[c], other_mid)
+        return remote(pair.at[c], from_mid.at[c], mid_send.at[0], mid_recv.at[c], other_mid)
 
     def to_end(c):
-        return remote(total.at[c], total.at[c], tot_send.at[c], tot_recv.at[c], near_end)
-
-    def first_pass(e, carry):
-        dy = mm(chosen[e], dy_all[...].reshape(tokens, width)).astype(jnp.bfloat16)
-        scaled[e] = (gate_rows[e][:, :1] * dy.astype(jnp.float32)).astype(jnp.bfloat16)
-        load(0, e).wait()
-        for h in range(per):
-            raw = mm_dims(dy, wd[e, h * piece : (h + 1) * piece, :], NT)
-            own[e * per + h] = raw.astype(jnp.bfloat16)
-
-            @pl.when(is_end)
-            def _():
-                to_mid(e * per + h).start()
-
-        save(1, e).start()
-        return carry
-
-    with jax.named_scope("first"):
-        lax.fori_loop(0, local, first_pass, 0)
+        return remote(total.at[c], total.at[c], end_send.at[0], end_recv.at[c], near_end)
 
     def join(c):
         to_mid(c).wait_recv()
         pair[c] = (own[c].astype(jnp.float32) + from_end[c].astype(jnp.float32)).astype(jnp.bfloat16)
         to_pair(c).start()
+
+    def pick_rows(e):
+        dy = mm(chosen[e * slots : (e + 1) * slots], dy_all[...].reshape(tokens, width)).astype(jnp.bfloat16)
+        dy_rows[e % 2] = dy
+        scaled[e] = (gate_rows[e][:, :1] * dy.astype(jnp.float32)).astype(jnp.bfloat16)
+
+    def first_pass(e):
+        if e == local - 1:
+            @pl.when(is_mid)
+            def _():
+                join(0)
+
+        if e + 1 < local:
+            pick_rows(e + 1)
+        cuts = per if e == 0 else 1
+        size = ff // cuts
+        each = per // cuts
+        for k in range(cuts):
+            raw = mm_dims(dy_rows[e % 2], wd[e, k * size : (k + 1) * size, :], NT)
+            raw = raw.astype(jnp.bfloat16)
+            lo = e * per + k * each
+            for h in range(each):
+                own[lo + h] = raw[:, h * piece : (h + 1) * piece]
+
+            @pl.when(is_end)
+            def _():
+                for h in range(each):
+                    to_mid(lo + h).start()
+
+    with jax.named_scope("first"):
+        loaded(0)
+        pick_rows(0)
+        for e in range(local):
+            first_pass(e)
+            save(1, e).start()
 
     def arrive(c):
         @pl.when(is_mid & (c + LAG < chunks))
@@ -403,96 +448,95 @@
             to_end(c).wait_recv()
 
     with jax.named_scope("lead"):
+        relay(x_all, x_send, x_recv)
+
         @pl.when(is_mid)
         def _():
-            for c in range(LAG):
+            for c in range(1, LAG):
                 join(c)
 
-        back_acc[...] = jnp.zeros_like(back_acc)
-        score_acc[...] = jnp.zeros_like(score_acc)
-
-    def place(e, carry):
-        rows_of = mm(chosen[e], x_all[...].reshape(tokens, width))
+        rest(x_all, x_send, x_recv)
+
+    def place(e):
+        rows_of = mm(chosen[e * slots : (e + 1) * slots], x_all[...].reshape(tokens, width))
         x_cols[e] = rows_of.T.astype(jnp.bfloat16)
         save(0, e).start()
-        return carry
+
+    with jax.named_scope("place"):
+        for e in range(local):
+            place(e)
+
+    wide = ff // STEPS
 
     def second_pass(e, carry):
-        for h in range(per):
-            c = e * per + h
+        for h in range(STEPS):
             with jax.named_scope("arrive"):
-                arrive(c)
+                for k in range(per // STEPS):
+                    arrive(e * per + h * (per // STEPS) + k)
 
             with jax.named_scope("dx"):
-                span = slice(h * piece, (h + 1) * piece)
-                raw = total[c].astype(jnp.float32)
+                span = slice(h * wide, (h + 1) * wide)
+                parts = [
+                    total[e * per + h * (per // STEPS) + k].astype(jnp.float32)
+                    for k in range(per // STEPS)
+                ]
+                raw = jnp.concatenate(parts, axis=1)
                 dh = gate_rows[e][:, :1] * raw
                 dg = (dh * to_gate[e, :, span]).astype(jnp.bfloat16)
                 du = (dh * to_up[e, :, span]).astype(jnp.bfloat16)
                 d_gate[e, :, span] = dg
                 d_up[e, :, span] = du
                 part = jnp.sum(raw * hidden[e, :, span].astype(jnp.float32), axis=1, keepdims=True)
+                part = jnp.broadcast_to(part, score_cols.shape)
                 if h == 0:
-                    score_cols[...] = jnp.broadcast_to(part, score_cols.shape)
+                    score_cols[...] = part
 
                     @pl.when(e == 0)
                     def _():
-                        for i in range(local):
-                            load(1, i).wait()
-                            load(2, i).wait()
+                        loaded(1)
+                        loaded(2)
                 else:
-                    score_cols[...] += part
+                    part = part + score_cols[...]
+                    score_cols[...] = part
                 dx = mm_dims(dg, wg[e, :, span], NT) + mm_dims(du, wu[e, :, span], NT)
-                if h == 0:
+                if h > 0:
+                    dx = dx + dx_acc[...]
+                if h < STEPS - 1:
                     dx_acc[...] = dx
                 else:
-                    dx_acc[...] += dx
-        with jax.named_scope("back"):
-            save(3, e).start()
-            save(4, e).start()
-            pick = chosen_t[e][:, :slots]
-            back_acc[...] += mm(pick, dx_acc[...].astype(jnp.bfloat16))
-            at = lax.broadcasted_iota(jnp.int32, (slots, LANES), 1)
-            score = jnp.where(at == e, score_cols[...], 0.0).astype(jnp.bfloat16)
-            score_acc[...] += mm(pick, score)
-
-        @pl.when(e == 0)
-        def _():
-            with jax.named_scope("xrelay"):
-                relay(x_all, x_send, x_recv)
-
-        @pl.when(e == 1)
-        def _():
-            with jax.named_scope("xplace"):
-                rest(x_all, x_send, x_recv)
-                lax.fori_loop(0, local, place, 0)
-
+                    dx_rows[e] = dx.astype(jnp.bfloat16)
+                    at = lax.broadcasted_iota(jnp.int32, (slots, LANES), 1)
+                    score_rows[e] = jnp.where(at == e, part, 0.0).astype(jnp.bfloat16)
+        save(3, e).start()
+        save(4, e).start()
         return carry
 
     lax.fori_loop(0, local, second_pass, 0)
+    with jax.named_scope("back"):
+        flat = dx_rows[...].reshape(local * slots, width)
+        sums = mm(chosen_t[...], flat).astype(jnp.bfloat16)
+        back[:, :, :width] = sums.reshape(groups, rows, width)
+        flat = score_rows[...].reshape(local * slots, LANES)
+        sums = mm(chosen_t[...], flat).astype(jnp.bfloat16)
+        back[:, :, width:] = sums.reshape(groups, rows, LANES)
     with jax.named_scope("finish"):
-        back[:, :, :width] = back_acc[...].astype(jnp.bfloat16).reshape(groups, rows, width)
-        back[:, :, width:] = score_acc[...].astype(jnp.bfloat16).reshape(groups, rows, LANES)
-        last = pltpu.make_async_copy(back, back_out, out_sem.at[5 * local])
+        last = pltpu.make_async_copy(back, back_out, out_sem.at[5])
         last.start()
-        drain(small, sm_all, sm_send, sm_recv)
-        drain(cot, dy_all, dy_send, dy_recv)
-        drain(tok, x_all, x_send, x_recv)
+        drain(sm_all, sm_send, sm_recv)
+        drain(dy_all, dy_send, dy_recv)
+        drain(x_all, x_send, x_recv)
 
         @pl.when(is_end)
         def _():
-            for c in range(chunks):
-                to_mid(c).wait_send()
+            remote(own, from_end, end_send.at[0], end_recv.at[0], near_mid).wait_send()
 
         @pl.when(is_mid)
         def _():
-            for c in range(chunks):
-                to_pair(c).wait_send()
-                to_end(c).wait_send()
+            remote(pair, from_mid, mid_send.at[0], mid_recv.at[0], other_mid).wait_send()
+            remote(total, total, end_send.at[0], end_recv.at[0], near_end).wait_send()
 
         for which in range(5):
-            for e in range(local):
-                save(which, e).wait()
+            pltpu.make_async_copy(*saves[which], out_sem.at[which]).wait()
         last.wait()
 
 
@@ -500,13 +544,11 @@
     rows, width = cot.shape
     local, slots, ff = act_gate.shape
     tokens = groups * rows
-    chunks = local * HALVES
-    piece = ff // HALVES
+    chunks = local * SPLIT
+    piece = ff // SPLIT
     n_ex, n_ey = lax.axis_size("ex"), lax.axis_size("ey")
     bf, f32 = jnp.bfloat16, jnp.float32
-    sends = 2 * n_ex - 1
     dma = pltpu.SemaphoreType.DMA
-    vmem = pl.BlockSpec(memory_space=pltpu.VMEM)
     hbm = pl.BlockSpec(memory_space=pltpu.HBM)
     buf = pltpu.VMEM((chunks, slots, piece), bf)
     outs = (
@@ -516,7 +558,7 @@
     return pl.pallas_call(
         functools.partial(exchange_kernel, cap),
         out_shape=tuple(jax.ShapeDtypeStruct(shape, bf) for shape in outs),
-        in_specs=[vmem] * 6 + [hbm] * 3,
+        in_specs=[hbm] * 9,
         out_specs=(hbm,) * 6,
         scratch_shapes=[
             pltpu.VMEM((2 * gates.shape[0], LANES), bf),
@@ -526,8 +568,8 @@
             pltpu.VMEM((local, ff, width), bf),
             pltpu.VMEM((local, width, ff), bf),
             pltpu.VMEM((local, width, ff), bf),
-            pltpu.VMEM((local, slots, tokens), bf),
-            pltpu.VMEM((local, tokens, LANES), bf),
+            pltpu.VMEM((local * slots, tokens), bf),
+            pltpu.VMEM((tokens, local * slots), bf),
             pltpu.VMEM((local, slots, LANES), f32),
             pltpu.VMEM((local, width, slots), bf),
             pltpu.VMEM((local, slots, width), bf),
@@ -540,16 +582,22 @@
             pltpu.VMEM((local, slots, ff), f32),
             buf, buf, buf, buf, buf,
             pltpu.VMEM((slots, width), f32),
-            pltpu.VMEM((tokens, width), f32),
-            pltpu.VMEM((tokens, LANES), f32),
+            pltpu.VMEM((local, slots, width), bf),
+            pltpu.VMEM((local, slots, LANES), bf),
             pltpu.VMEM((slots, LANES), f32),
-            dma((3 * local,)), dma((5 * local + 1,)),
-            dma((sends,)), dma((groups,)),
-            dma((sends,)), dma((groups,)),
-            dma((sends,)), dma((groups,)),
-            dma((chunks,)), dma((chunks,)),
-            dma((chunks,)), dma((chunks,)),
-            dma((chunks,)), dma((chunks,)),
+            pltpu.VMEM((2, slots, width), bf),
+            pltpu.VMEM((local, slots, ff), bf),
+            pltpu.VMEM((local, slots, ff), bf),
+            pltpu.VMEM(gates.shape, bf),
+            pltpu.VMEM(ids.shape, jnp.int32),
+            pltpu.VMEM((rows, width), bf),
+            pltpu.VMEM((rows, width), bf),
+            dma((3,)), dma((2,)), dma((4,)), dma((6,)),
+            dma((1,)), dma((n_ex,)),
+            dma((1,)), dma((n_ex,)),
+            dma((1,)), dma((n_ex,)),
+            dma((1,)), dma((chunks,)),
+            dma((1,)), dma((chunks,)),
         ],
         compiler_params=pltpu.CompilerParams(
             collective_id=0, has_side_effects=True, vmem_limit_bytes=63 << 20
@@ -576,9 +624,9 @@
     def save(which, e, j):
         src = (down, gate, up)[which]
         dst = (down_out, gate_out, up_out)[which]
-        at = pl.ds(pl.multiple_of(j * tile, tile), tile)
+        at = slice(j * tile, (j + 1) * tile)
         index = (e, slice(None), at) if which == 0 else (e, at)
-        return pltpu.make_async_copy(src.at[index], dst.at[index], out_sem.at[which, e * steps + j])
+        return pltpu.make_async_copy(src.at[index], dst.at[index], out_sem.at[which])
 
     for e in range(local):
         for which in range(5):
@@ -588,8 +636,8 @@
         for which in range(5):
             load(which, e).wait()
 
-        def step(j, carry):
-            at = pl.ds(pl.multiple_of(j * tile, tile), tile)
+        for j in range(steps):
+            at = slice(j * tile, (j + 1) * tile)
             x_t = x_cols[e, at, :]
             gate[e, at, :] = mm(x_t, d_gate[e]).astype(jnp.bfloat16)
             save(1, e, j).start()
@@ -597,19 +645,12 @@
             save(2, e, j).start()
             down[e, :, at] = mm(hidden[e], scaled[e, :, at]).astype(jnp.bfloat16)
             save(0, e, j).start()
-            return carry
-
-        return lax.fori_loop(0, steps, step, carry)
+        return carry
 
     lax.fori_loop(0, local, expert, 0)
 
-    def finish(e, carry):
-        for which in range(3):
-            for j in range(steps):
-                save(which, e, j).wait()
-        return carry
-
-    lax.fori_loop(0, local, finish, 0)
+    for which, (src, dst) in enumerate(((down, down_out), (gate, gate_out), (up, up_out))):
+        pltpu.make_async_copy(src, dst, out_sem.at[which]).wait()
 
 
 def weight_grads(x_cols, scaled, hidden, d_gate, d_up):
@@ -627,7 +668,7 @@
         out_specs=(hbm,) * 3,
         scratch_shapes=ins
         + [pltpu.VMEM(shape, bf) for shape in outs]
-        + [dma((5, local)), dma((3, local * (width // 256)))],
+        + [dma((5, local)), dma((3,))],
         compiler_params=pltpu.CompilerParams(vmem_limit_bytes=60 << 20),
         cost_estimate=pl.CostEstimate(
             flops=6 * local * slots * ff * width,
@@ -651,11 +692,11 @@
     back = lax.all_to_all(back, GROUP, split_axis=0, concat_axis=0, tiled=True)
     grad_w_down, grad_w_gate, grad_w_up = weight_grads(x_cols, scaled, hidden, d_gate, d_up)
     grad_tokens = jnp.sum(back[:, :, :width].astype(jnp.float32), axis=0).astype(jnp.bfloat16)
-    table = back[:, :, width : width + local].transpose(1, 0, 2).reshape(rows, groups * local)
-    picks = expert_ids[:, :, None] == jnp.arange(groups * local, dtype=jnp.int32)[None, None, :]
-    grad_gates = jnp.sum(
-        jnp.where(picks, table.astype(jnp.float32)[:, None, :], 0.0), axis=2
-    ).astype(jnp.bfloat16)
+    table = back[:, :, width : width + local].transpose(0, 2, 1).astype(jnp.float32)
+    names = jnp.arange(groups * local, dtype=jnp.int32).reshape(groups, local, 1, 1)
+    picks = expert_ids.T[None, None] == names
+    grad_gates = jnp.sum(jnp.where(picks, table[:, :, None, :], 0.0), axis=(0, 1))
+    grad_gates = grad_gates.astype(jnp.bfloat16).T
     return (grad_tokens, grad_gates, grad_w_gate, grad_w_up, grad_w_down)
 
 

time: 70.8 us -> 64.1 us (0.905)
  Pallas kernels: 63.8 us -> 58.1 us
  local copies, waits for them, and re-layouts: 1.61 us -> 0.12 us
    pallas_call x1, Pallas kernels: 45.4 us -> 42.3 us  [exchange(): pl.pallas_call(functools.partial(exchange_kernel, cap), out_shape=tuple((...]
    pallas_call x1, Pallas kernels: 18.4 us -> 15.8 us  [weight_grads(): pl.pallas_call(weights_kernel, out_shape=tuple((jax.ShapeDtypeStruct(shap...]
    unnamed x2, local copies, waits for them, and re-layouts: 1.43 us -> 0.01 us
  transfers between devices with their start and end apart: 1 -> 1, of which waited for: 0 -> 0; matrix products, arithmetic and copies ran while one was open for 1% -> 0% of each run, Pallas kernels for 26% -> 25%
where the time goes in v2:
time: 64.1 us; the launch traced here: 63.9 us
  Pallas kernels  58.1 us (91%)
  starting transfers between devices  3.57 us (6%)
  other arithmetic  1.48 us (2%)
  between operations  0.69 us (1%)
    pallas_call x1, Pallas kernels, exchange(): pl.pallas_call(functools.partial(exchange_kernel, cap), out_shape=tuple((...  42.3 us
    pallas_call x1, Pallas kernels, weight_grads(): pl.pallas_call(weights_kernel, out_shape=tuple((jax.ShapeDtypeStruct(shap...  15.8 us
    all_to_all x1, starting transfers between devices, on_device(): back = lax.all_to_all(back, GROUP, split_axis=0, concat_axis=0, tiled=True)  3.57 us
  transfers between devices with their start and end apart: 1, of which 0 were waited for; matrix products, arithmetic and copies ran while one was open for 0% of the time, Pallas kernels for 25%

profile of v2, /device:TPU:0, one launch (start us, length us, event | category | flops | bytes accessed | tf_op | source)
XLA Modules:
  0.0 63.9 jit_solution(14360753320507193150)
XLA Ops:
  0.6 42.3 %exchange.1 = (bf16[4,1792,80]{2,1,0:T(8,128)(2,1)}, bf16[4,80,1792]{2,1,0:T(8,128)(2,1)}, bf16[4,1024,80]{2,1,0:T(8,128)(2,1)}, bf16[4,80,1024]{2,1,0:T(8,128)(...) custom-call(bf16[8,32]{1,0:T(8,128)(2,1)} %bitcast.14, s32[8,32]{1,0:T(8,128)} %bitcast.11, ...), custom_call_target="tpu_custom_call" | custom-call | tf_op jit(solution)/shard_map/exchange/pallas_call | solution.py:558
  43.0 0.0 copy-start
  43.0 3.6 %all-to-all-start = ((bf16[8,32,1920]{2,1,0:T(8,128)(2,1)}), bf16[8,32,1920]{2,1,0:T(8,128)(2,1)S(1)}, u32[]{:S(2)}, u32[]{:S(2)}) async-start(bf16[8,32,1920]{2,1,0:T(8,128)(2,1)} %get-tuple-element.14), calls=%async_computation | async-start | bytes 1966080 | tf_op jit(solution)/shard_map/all_to_all | solution.py:692
  46.6 15.8 %weight_grads.1 = (bf16[4,1024,1792]{2,1,0:T(8,128)(2,1)}, bf16[4,1792,1024]{2,1,0:T(8,128)(2,1)}, bf16[4,1792,1024]{2,1,0:T(8,128)(2,1)}) custom-call(bf16[4,1792,80]{2,1,0:T(8,128)(2,1)} %get-tuple-element.15.x_cols_in, bf16[4,80,1792]{2,1,0:T(8,128)(2,1)} %get-tuple-element.16.scaled_in, bf16[4,1024,80]{2,1,0:T(8,128)(2,1)} %get-tuple-element.17.hidden_in, ...), custom_call_target="tpu_custom_call" | custom-call | flops 3523215360 | bytes 44040192 | tf_op jit(solution)/shard_map/weight_grads/pallas_call | solution.py:664
  62.3 0.0 all-to-all-done
  62.4 0.1 copy.15
  62.5 0.0 copy-done
  62.5 0.7 %select_reduce_fusion = bf16[8,32]{1,0:T(8,128)(2,1)} fusion(f32[8,4,32]{2,1,0:T(4,128)S(1)} %copy.15, s32[8,4]{1,0:T(8,128)S(1)} %multiply_add_fusion, s32[8,32]{1,0:T(8,128)S(1)} %bitcast.12), kind=kLoop, calls=%fused_computation.2 | loop fusion | flops 24320 | bytes 5760 | tf_op jit(solution)/shard_map/reduce_sum | solution.py:698
  63.2 0.8 %slice_reduce_fusion = bf16[32,1792]{1,0:T(8,128)(2,1)} fusion(bf16[8,32,1920]{2,1,0:T(8,128)(2,1)S(1)} %all-to-all-done), kind=kLoop, calls=%fused_computation | loop fusion | flops 401408 | bytes 1032192 | tf_op jit(solution)/shard_map/reduce_sum | solution.py:694
  (2 shorter events, 0.0 us)
Async XLA Ops:
  43.0 19.5 %copy-start = (s32[32,8]{0,1:T(8,128)S(1)}, s32[32,8]{0,1:T(8,128)}, u32[]{:S(2)}) copy-start(s32[32,8]{0,1:T(8,128)} %param.12) | copy-start | bytes 3076
  43.0 19.4 %all-to-all-start = ((bf16[8,32,1920]{2,1,0:T(8,128)(2,1)}), bf16[8,32,1920]{2,1,0:T(8,128)(2,1)S(1)}, u32[]{:S(2)}, u32[]{:S(2)}) async-start(bf16[8,32,1920]{2,1,0:T(8,128)(2,1)} %get-tuple-element.14), calls=%async_computation | async-start | bytes 1966080 | tf_op jit(solution)/shard_map/all_to_all | solution.py:692

commit v3 on v2

--- a/solution.py
+++ b/solution.py
@@ -180,9 +180,9 @@
 def exchange_kernel(
     cap,
     gates_hbm, ids_hbm, cot_hbm, tok_hbm, gate_in, up_in, w_gate, w_up, w_down,
-    x_cols_out, scaled_out, hidden_out, d_gate_out, d_up_out, back_out,
+    x_out, scaled_out, hidden, d_gate, d_up, back,
     small, dy_all, x_all, sm_all, wd, wg, wu, chosen, chosen_t, gate_rows,
-    x_cols, scaled, hidden_t, hidden, d_gate, d_up, back, to_gate, to_up,
+    x_rows, scaled, to_gate, to_up,
     own, from_end, pair, from_mid, total, dx_acc, dx_rows, score_rows, score_cols,
     dy_rows, act_gate, act_up, gates_in, ids_in, cot, tok,
     w_sem, act_sem, head_sem, out_sem, dy_send, dy_recv, x_send, x_recv, sm_send, sm_recv,
@@ -218,10 +218,7 @@
         dst = (wd, wg, wu)[which]
         pltpu.make_async_copy(src, dst, w_sem.at[which]).wait()
 
-    saves = (
-        (x_cols, x_cols_out), (scaled, scaled_out), (hidden_t, hidden_out),
-        (d_gate, d_gate_out), (d_up, d_up_out),
-    )
+    saves = ((scaled, scaled_out), (x_rows, x_out))
 
     def save(which, e):
         src, dst = saves[which]
@@ -312,10 +309,8 @@
         silu = a * q
         hid = silu * u
         hidden[e] = hid.astype(jnp.bfloat16)
-        hidden_t[e] = hid.T.astype(jnp.bfloat16)
         to_gate[e] = u * q * (1.0 + a * (1.0 - q))
         to_up[e] = silu
-        save(2, e).start()
         return carry
 
     sm_all[group] = small[...]
@@ -429,7 +424,7 @@
         pick_rows(0)
         for e in range(local):
             first_pass(e)
-            save(1, e).start()
+            save(0, e).start()
 
     def arrive(c):
         @pl.when(is_mid & (c + LAG < chunks))
@@ -459,8 +454,8 @@
 
     def place(e):
         rows_of = mm(chosen[e * slots : (e + 1) * slots], x_all[...].reshape(tokens, width))
-        x_cols[e] = rows_of.T.astype(jnp.bfloat16)
-        save(0, e).start()
+        x_rows[e] = rows_of.astype(jnp.bfloat16)
+        save(1, e).start()
 
     with jax.named_scope("place"):
         for e in range(local):
@@ -507,8 +502,6 @@
                     dx_rows[e] = dx.astype(jnp.bfloat16)
                     at = lax.broadcasted_iota(jnp.int32, (slots, LANES), 1)
                     score_rows[e] = jnp.where(at == e, part, 0.0).astype(jnp.bfloat16)
-        save(3, e).start()
-        save(4, e).start()
         return carry
 
     lax.fori_loop(0, local, second_pass, 0)
@@ -520,8 +513,8 @@
         sums = mm(chosen_t[...], flat).astype(jnp.bfloat16)
         back[:, :, width:] = sums.reshape(groups, rows, LANES)
     with jax.named_scope("finish"):
-        last = pltpu.make_async_copy(back, back_out, out_sem.at[5])
-        last.start()
+        for which in range(2):
+            pltpu.make_async_copy(*saves[which], out_sem.at[which]).wait()
         drain(sm_all, sm_send, sm_recv)
         drain(dy_all, dy_send, dy_recv)
         drain(x_all, x_send, x_recv)
@@ -534,10 +527,6 @@
         def _():
             remote(pair, from_mid, mid_send.at[0], mid_recv.at[0], other_mid).wait_send()
             remote(total, total, end_send.at[0], end_recv.at[0], near_end).wait_send()
-
-        for which in range(5):
-            pltpu.make_async_copy(*saves[which], out_sem.at[which]).wait()
-        last.wait()
 
 
 def exchange(cap, groups, gates, ids, cot, tok, act_gate, act_up, w_gate, w_up, w_down):
@@ -551,15 +540,20 @@
     dma = pltpu.SemaphoreType.DMA
     hbm = pl.BlockSpec(memory_space=pltpu.HBM)
     buf = pltpu.VMEM((chunks, slots, piece), bf)
+    vmem = pl.BlockSpec(memory_space=pltpu.VMEM)
     outs = (
-        (local, width, slots), (local, slots, width), (local, ff, slots),
+        (local, slots, width), (local, slots, width), (local, slots, ff),
         (local, slots, ff), (local, slots, ff), (groups, rows, width + LANES),
     )
+    kept = [
+        pltpu.VMEM(shape, bf) if 2 <= i < 5 else jax.ShapeDtypeStruct(shape, bf)
+        for i, shape in enumerate(outs)
+    ]
     return pl.pallas_call(
         functools.partial(exchange_kernel, cap),
-        out_shape=tuple(jax.ShapeDtypeStruct(shape, bf) for shape in outs),
+        out_shape=tuple(kept),
         in_specs=[hbm] * 9,
-        out_specs=(hbm,) * 6,
+        out_specs=(hbm, hbm, vmem, vmem, vmem, vmem),
         scratch_shapes=[
             pltpu.VMEM((2 * gates.shape[0], LANES), bf),
             pltpu.VMEM((groups, rows, width), bf),
@@ -571,13 +565,8 @@
             pltpu.VMEM((local * slots, tokens), bf),
             pltpu.VMEM((tokens, local * slots), bf),
             pltpu.VMEM((local, slots, LANES), f32),
-            pltpu.VMEM((local, width, slots), bf),
             pltpu.VMEM((local, slots, width), bf),
-            pltpu.VMEM((local, ff, slots), bf),
-            pltpu.VMEM((local, slots, ff), bf),
-            pltpu.VMEM((local, slots, ff), bf),
-            pltpu.VMEM((local, slots, ff), bf),
-            pltpu.VMEM((groups, rows, width + LANES), bf),
+            pltpu.VMEM((local, slots, width), bf),
             pltpu.VMEM((local, slots, ff), f32),
             pltpu.VMEM((local, slots, ff), f32),
             buf, buf, buf, buf, buf,
@@ -592,7 +581,7 @@
             pltpu.VMEM(ids.shape, jnp.int32),
             pltpu.VMEM((rows, width), bf),
             pltpu.VMEM((rows, width), bf),
-            dma((3,)), dma((2,)), dma((4,)), dma((6,)),
+            dma((3,)), dma((2,)), dma((4,)), dma((2,)),
             dma((1,)), dma((n_ex,)),
             dma((1,)), dma((n_ex,)),
             dma((1,)), dma((n_ex,)),
@@ -600,26 +589,19 @@
             dma((1,)), dma((chunks,)),
         ],
         compiler_params=pltpu.CompilerParams(
-            collective_id=0, has_side_effects=True, vmem_limit_bytes=63 << 20
+            collective_id=0, has_side_effects=True, vmem_limit_bytes=60 << 20
         ),
         name="exchange",
     )(gates, ids, cot, tok, act_gate, act_up, w_gate, w_up, w_down)
 
 
 def weights_kernel(
-    x_cols_in, scaled_in, hidden_in, d_gate_in, d_up_in,
-    down_out, gate_out, up_out,
-    x_cols, scaled, hidden, d_gate, d_up, down, gate, up, in_sem, out_sem,
+    x_in, scaled_in, hidden, d_gate, d_up,
+    down_out, gate_out, up_out, x_rows, scaled, x_cols, hid_cols, down, gate, up, in_sem, out_sem,
 ):
-    local, width, slots = x_cols.shape
-    ff = hidden.shape[1]
+    local, slots, width = x_rows.shape
     tile = 256
     steps = width // tile
-
-    def load(which, e):
-        src = (hidden_in, scaled_in, x_cols_in, d_gate_in, d_up_in)[which]
-        dst = (hidden, scaled, x_cols, d_gate, d_up)[which]
-        return pltpu.make_async_copy(src.at[e], dst.at[e], in_sem.at[which, e])
 
     def save(which, e, j):
         src = (down, gate, up)[which]
@@ -628,55 +610,62 @@
         index = (e, slice(None), at) if which == 0 else (e, at)
         return pltpu.make_async_copy(src.at[index], dst.at[index], out_sem.at[which])
 
+    def load(which, e):
+        src = (scaled_in, x_in)[which]
+        dst = (scaled, x_rows)[which]
+        return pltpu.make_async_copy(src.at[e], dst.at[e], in_sem.at[which, e])
+
     for e in range(local):
-        for which in range(5):
+        for which in range(2):
             load(which, e).start()
 
+    def flip(e):
+        hid_cols[...] = hidden[e].astype(jnp.float32).T.astype(jnp.bfloat16)
+        load(0, e).wait()
+        load(1, e).wait()
+        x_cols[...] = x_rows[e].astype(jnp.float32).T.astype(jnp.bfloat16)
+
     def expert(e, carry):
-        for which in range(5):
-            load(which, e).wait()
-
+        flip(e)
         for j in range(steps):
             at = slice(j * tile, (j + 1) * tile)
-            x_t = x_cols[e, at, :]
+            x_t = x_cols[at, :]
             gate[e, at, :] = mm(x_t, d_gate[e]).astype(jnp.bfloat16)
             save(1, e, j).start()
             up[e, at, :] = mm(x_t, d_up[e]).astype(jnp.bfloat16)
             save(2, e, j).start()
-            down[e, :, at] = mm(hidden[e], scaled[e, :, at]).astype(jnp.bfloat16)
+            down[e, :, at] = mm(hid_cols[...], scaled[e, :, at]).astype(jnp.bfloat16)
             save(0, e, j).start()
         return carry
 
     lax.fori_loop(0, local, expert, 0)
-
     for which, (src, dst) in enumerate(((down, down_out), (gate, gate_out), (up, up_out))):
         pltpu.make_async_copy(src, dst, out_sem.at[which]).wait()
 
 
-def weight_grads(x_cols, scaled, hidden, d_gate, d_up):
-    local, width, slots = x_cols.shape
-    ff = hidden.shape[1]
+def weight_grads(x_rows, scaled, hidden, d_gate, d_up):
+    local, slots, width = x_rows.shape
+    ff = hidden.shape[2]
     bf = jnp.bfloat16
     hbm = pl.BlockSpec(memory_space=pltpu.HBM)
+    vmem = pl.BlockSpec(memory_space=pltpu.VMEM)
     outs = ((local, ff, width), (local, width, ff), (local, width, ff))
-    ins = [pltpu.VMEM(part.shape, bf) for part in (x_cols, scaled, hidden, d_gate, d_up)]
-    dma = pltpu.SemaphoreType.DMA
     return pl.pallas_call(
         weights_kernel,
         out_shape=tuple(jax.ShapeDtypeStruct(shape, bf) for shape in outs),
-        in_specs=[hbm] * 5,
+        in_specs=[hbm, hbm, vmem, vmem, vmem],
         out_specs=(hbm,) * 3,
-        scratch_shapes=ins
+        scratch_shapes=[pltpu.VMEM(scaled.shape, bf), pltpu.VMEM(scaled.shape, bf), pltpu.VMEM((width, slots), bf), pltpu.VMEM((ff, slots), bf)]
         + [pltpu.VMEM(shape, bf) for shape in outs]
-        + [dma((5, local)), dma((3,))],
-        compiler_params=pltpu.CompilerParams(vmem_limit_bytes=60 << 20),
+        + [pltpu.SemaphoreType.DMA((2, local)), pltpu.SemaphoreType.DMA((3,))],
+        compiler_params=pltpu.CompilerParams(vmem_limit_bytes=52 << 20),
         cost_estimate=pl.CostEstimate(
             flops=6 * local * slots * ff * width,
             bytes_accessed=6 * local * ff * width,
             transcendentals=0,
         ),
         name="weight_grads",
-    )(x_cols, scaled, hidden, d_gate, d_up)
+    )(x_rows, scaled, hidden, d_gate, d_up)
 
 
 def on_device(tokens, cotangent, gates, expert_ids, saved_gate, saved_up, w_gate, w_up, w_down):
@@ -685,12 +674,12 @@
     local, slots = saved_gate.shape[1:]
     act_gate = saved_gate.transpose(1, 2, 0)
     act_up = saved_up.transpose(1, 2, 0)
-    x_cols, scaled, hidden, d_gate, d_up, back = exchange(
+    x_rows, scaled, hidden, d_gate, d_up, back = exchange(
         slots // groups, groups, gates.T, expert_ids.T, cotangent, tokens,
         act_gate, act_up, w_gate, w_up, w_down,
     )
     back = lax.all_to_all(back, GROUP, split_axis=0, concat_axis=0, tiled=True)
-    grad_w_down, grad_w_gate, grad_w_up = weight_grads(x_cols, scaled, hidden, d_gate, d_up)
+    grad_w_down, grad_w_gate, grad_w_up = weight_grads(x_rows, scaled, hidden, d_gate, d_up)
     grad_tokens = jnp.sum(back[:, :, :width].astype(jnp.float32), axis=0).astype(jnp.bfloat16)
     table = back[:, :, width : width + local].transpose(0, 2, 1).astype(jnp.float32)
     names = jnp.arange(groups * local, dtype=jnp.int32).reshape(groups, local, 1, 1)

time: 64.1 us -> 62.9 us (0.981)
  Pallas kernels: 58.1 us -> 56.9 us
    pallas_call x1, Pallas kernels: 42.3 us -> 41.4 us  [exchange(): pl.pallas_call(functools.partial(exchange_kernel, cap), out_shape=tuple(k...]
where the time goes in v3:
time: 62.9 us; the launch traced here: 62.7 us
  Pallas kernels  56.9 us (90%)
  starting transfers between devices  3.57 us (6%)
  other arithmetic  1.48 us (2%)
  between operations  0.69 us (1%)
    pallas_call x1, Pallas kernels, exchange(): pl.pallas_call(functools.partial(exchange_kernel, cap), out_shape=tuple(k...  41.4 us
    pallas_call x1, Pallas kernels, weight_grads(): pl.pallas_call(weights_kernel, out_shape=tuple((jax.ShapeDtypeStruct(shap...  15.5 us
    all_to_all x1, starting transfers between devices, on_device(): back = lax.all_to_all(back, GROUP, split_axis=0, concat_axis=0, tiled=True)  3.57 us
  transfers between devices with their start and end apart: 1, of which 0 were waited for; matrix products, arithmetic and copies ran while one was open for 0% of the time, Pallas kernels for 25%

profile of v3, /device:TPU:0, one launch (start us, length us, event | category | flops | bytes accessed | tf_op | source)
XLA Modules:
  0.0 62.7 jit_solution(10484523631746952782)
XLA Ops:
  0.6 41.4 %exchange.1 = (bf16[4,80,1792]{2,1,0:T(8,128)(2,1)}, bf16[4,80,1792]{2,1,0:T(8,128)(2,1)}, bf16[4,80,1024]{2,1,0:T(8,128)(2,1)S(1)}, bf16[4,80,1024]{2,1,0:T(8,1...) custom-call(bf16[8,32]{1,0:T(8,128)(2,1)} %bitcast.14, s32[8,32]{1,0:T(8,128)} %bitcast.11, ...), custom_call_target="tpu_custom_call" | custom-call | tf_op jit(solution)/shard_map/exchange/pallas_call | solution.py:552
  42.0 0.0 copy-start
  42.0 3.6 %all-to-all-start = ((bf16[8,32,1920]{2,1,0:T(8,128)(2,1)}), bf16[8,32,1920]{2,1,0:T(8,128)(2,1)S(1)}, u32[]{:S(2)}, u32[]{:S(2)}) async-start(bf16[8,32,1920]{2,1,0:T(8,128)(2,1)} %get-tuple-element.14), calls=%async_computation | async-start | bytes 1966080 | tf_op jit(solution)/shard_map/all_to_all | solution.py:681
  45.6 15.5 %weight_grads.1 = (bf16[4,1024,1792]{2,1,0:T(8,128)(2,1)}, bf16[4,1792,1024]{2,1,0:T(8,128)(2,1)}, bf16[4,1792,1024]{2,1,0:T(8,128)(2,1)}) custom-call(bf16[4,80,1792]{2,1,0:T(8,128)(2,1)} %get-tuple-element.15.x_in, bf16[4,80,1792]{2,1,0:T(8,128)(2,1)} %get-tuple-element.16.scaled_in, bf16[4,80,1024]{2,1,0:T(8,128)(2,1)S(1)} %get-tuple-element.17.hidden, ...), custom_call_target="tpu_custom_call" | custom-call | flops 3523215360 | bytes 44040192 | tf_op jit(solution)/shard_map/weight_grads/pallas_call | solution.py:653
  61.1 0.0 all-to-all-done
  61.1 0.1 copy.15
  61.3 0.0 copy-done
  61.3 0.7 %select_reduce_fusion = bf16[8,32]{1,0:T(8,128)(2,1)} fusion(f32[8,4,32]{2,1,0:T(4,128)S(1)} %copy.15, s32[8,4]{1,0:T(8,128)S(1)} %multiply_add_fusion, s32[8,32]{1,0:T(8,128)S(1)} %bitcast.12), kind=kLoop, calls=%fused_computation.2 | loop fusion | flops 24320 | bytes 5760 | tf_op jit(solution)/shard_map/reduce_sum | solution.py:687
  62.0 0.8 %slice_reduce_fusion = bf16[32,1792]{1,0:T(8,128)(2,1)} fusion(bf16[8,32,1920]{2,1,0:T(8,128)(2,1)S(1)} %all-to-all-done), kind=kLoop, calls=%fused_computation | loop fusion | flops 401408 | bytes 1032192 | tf_op jit(solution)/shard_map/reduce_sum | solution.py:683
  (2 shorter events, 0.0 us)
Async XLA Ops:
  42.0 19.2 %copy-start = (s32[32,8]{0,1:T(8,128)S(1)}, s32[32,8]{0,1:T(8,128)}, u32[]{:S(2)}) copy-start(s32[32,8]{0,1:T(8,128)} %param.12) | copy-start | bytes 3076
  42.0 19.1 %all-to-all-start = ((bf16[8,32,1920]{2,1,0:T(8,128)(2,1)}), bf16[8,32,1920]{2,1,0:T(8,128)(2,1)S(1)}, u32[]{:S(2)}, u32[]{:S(2)}) async-start(bf16[8,32,1920]{2,1,0:T(8,128)(2,1)} %get-tuple-element.14), calls=%async_computation | async-start | bytes 1966080 | tf_op jit(solution)/shard_map/all_to_all | solution.py:681

commit v4 on v3

--- a/solution.py
+++ b/solution.py
@@ -180,9 +180,9 @@
 def exchange_kernel(
     cap,
     gates_hbm, ids_hbm, cot_hbm, tok_hbm, gate_in, up_in, w_gate, w_up, w_down,
-    x_out, scaled_out, hidden, d_gate, d_up, back,
+    x_out, scaled_out, hidden, d_gate, d_up, back_out,
     small, dy_all, x_all, sm_all, wd, wg, wu, chosen, chosen_t, gate_rows,
-    x_rows, scaled, to_gate, to_up,
+    x_rows, scaled, back, to_gate, to_up,
     own, from_end, pair, from_mid, total, dx_acc, dx_rows, score_rows, score_cols,
     dy_rows, act_gate, act_up, gates_in, ids_in, cot, tok,
     w_sem, act_sem, head_sem, out_sem, dy_send, dy_recv, x_send, x_recv, sm_send, sm_recv,
@@ -506,12 +506,17 @@
 
     lax.fori_loop(0, local, second_pass, 0)
     with jax.named_scope("back"):
-        flat = dx_rows[...].reshape(local * slots, width)
-        sums = mm(chosen_t[...], flat).astype(jnp.bfloat16)
-        back[:, :, :width] = sums.reshape(groups, rows, width)
-        flat = score_rows[...].reshape(local * slots, LANES)
-        sums = mm(chosen_t[...], flat).astype(jnp.bfloat16)
-        back[:, :, width:] = sums.reshape(groups, rows, LANES)
+        middle = width // 2 // LANES * LANES
+        bounds = (width, width + LANES), (0, middle), (middle, width)
+        sent = []
+        for n, (lo, hi) in enumerate(bounds):
+            source = score_rows[...] if lo == width else dx_rows[:, :, lo:hi]
+            flat = source.reshape(local * slots, hi - lo)
+            sums = mm(chosen_t[...], flat).astype(jnp.bfloat16)
+            back[:, :, lo:hi] = sums.reshape(groups, rows, hi - lo)
+            part = (slice(None), slice(None), slice(lo, hi))
+            sent.append(pltpu.make_async_copy(back.at[part], back_out.at[part], out_sem.at[2 + n]))
+            sent[-1].start()
     with jax.named_scope("finish"):
         for which in range(2):
             pltpu.make_async_copy(*saves[which], out_sem.at[which]).wait()
@@ -527,6 +532,9 @@
         def _():
             remote(pair, from_mid, mid_send.at[0], mid_recv.at[0], other_mid).wait_send()
             remote(total, total, end_send.at[0], end_recv.at[0], near_end).wait_send()
+
+        for copy in sent:
+            copy.wait()
 
 
 def exchange(cap, groups, gates, ids, cot, tok, act_gate, act_up, w_gate, w_up, w_down):
@@ -553,7 +561,7 @@
         functools.partial(exchange_kernel, cap),
         out_shape=tuple(kept),
         in_specs=[hbm] * 9,
-        out_specs=(hbm, hbm, vmem, vmem, vmem, vmem),
+        out_specs=(hbm, hbm, vmem, vmem, vmem, hbm),
         scratch_shapes=[
             pltpu.VMEM((2 * gates.shape[0], LANES), bf),
             pltpu.VMEM((groups, rows, width), bf),
@@ -567,6 +575,7 @@
             pltpu.VMEM((local, slots, LANES), f32),
             pltpu.VMEM((local, slots, width), bf),
             pltpu.VMEM((local, slots, width), bf),
+            pltpu.VMEM((groups, rows, width + LANES), bf),
             pltpu.VMEM((local, slots, ff), f32),
             pltpu.VMEM((local, slots, ff), f32),
             buf, buf, buf, buf, buf,
@@ -581,7 +590,7 @@
             pltpu.VMEM(ids.shape, jnp.int32),
             pltpu.VMEM((rows, width), bf),
             pltpu.VMEM((rows, width), bf),
-            dma((3,)), dma((2,)), dma((4,)), dma((2,)),
+            dma((3,)), dma((2,)), dma((4,)), dma((5,)),
             dma((1,)), dma((n_ex,)),
             dma((1,)), dma((n_ex,)),
             dma((1,)), dma((n_ex,)),

time: 62.9 us -> 62.8 us (level)
  no operation moved by 1% of the time
where the time goes in v4:
time: 62.8 us; the launch traced here: 62.6 us
  Pallas kernels  56.8 us (90%)
  starting transfers between devices  3.57 us (6%)
  other arithmetic  1.48 us (2%)
  between operations  0.69 us (1%)
    pallas_call x1, Pallas kernels, exchange(): pl.pallas_call(functools.partial(exchange_kernel, cap), out_shape=tuple(k...  41.3 us
    pallas_call x1, Pallas kernels, weight_grads(): pl.pallas_call(weights_kernel, out_shape=tuple((jax.ShapeDtypeStruct(shap...  15.5 us
    all_to_all x1, starting transfers between devices, on_device(): back = lax.all_to_all(back, GROUP, split_axis=0, concat_axis=0, tiled=True)  3.57 us
  transfers between devices with their start and end apart: 1, of which 0 were waited for; matrix products, arithmetic and copies ran while one was open for 0% of the time, Pallas kernels for 25%

profile of v4, /device:TPU:0, one launch (start us, length us, event | category | flops | bytes accessed | tf_op | source)
XLA Modules:
  0.0 62.6 jit_solution(2584672645661650510)
XLA Ops:
  0.6 41.3 %exchange.1 = (bf16[4,80,1792]{2,1,0:T(8,128)(2,1)}, bf16[4,80,1792]{2,1,0:T(8,128)(2,1)}, bf16[4,80,1024]{2,1,0:T(8,128)(2,1)S(1)}, bf16[4,80,1024]{2,1,0:T(8,1...) custom-call(bf16[8,32]{1,0:T(8,128)(2,1)} %bitcast.14, s32[8,32]{1,0:T(8,128)} %bitcast.11, ...), custom_call_target="tpu_custom_call" | custom-call | tf_op jit(solution)/shard_map/exchange/pallas_call | solution.py:560
  41.9 0.0 copy-start
  41.9 3.6 %all-to-all-start = ((bf16[8,32,1920]{2,1,0:T(8,128)(2,1)}), bf16[8,32,1920]{2,1,0:T(8,128)(2,1)S(1)}, u32[]{:S(2)}, u32[]{:S(2)}) async-start(bf16[8,32,1920]{2,1,0:T(8,128)(2,1)} %get-tuple-element.14), calls=%async_computation | async-start | bytes 1966080 | tf_op jit(solution)/shard_map/all_to_all | solution.py:690
  45.5 15.5 %weight_grads.1 = (bf16[4,1024,1792]{2,1,0:T(8,128)(2,1)}, bf16[4,1792,1024]{2,1,0:T(8,128)(2,1)}, bf16[4,1792,1024]{2,1,0:T(8,128)(2,1)}) custom-call(bf16[4,80,1792]{2,1,0:T(8,128)(2,1)} %get-tuple-element.15.x_in, bf16[4,80,1792]{2,1,0:T(8,128)(2,1)} %get-tuple-element.16.scaled_in, bf16[4,80,1024]{2,1,0:T(8,128)(2,1)S(1)} %get-tuple-element.17.hidden, ...), custom_call_target="tpu_custom_call" | custom-call | flops 3523215360 | bytes 44040192 | tf_op jit(solution)/shard_map/weight_grads/pallas_call | solution.py:662
  61.0 0.0 all-to-all-done
  61.0 0.1 copy.15
  61.1 0.0 copy-done
  61.1 0.7 %select_reduce_fusion = bf16[8,32]{1,0:T(8,128)(2,1)} fusion(f32[8,4,32]{2,1,0:T(4,128)S(1)} %copy.15, s32[8,4]{1,0:T(8,128)S(1)} %multiply_add_fusion, s32[8,32]{1,0:T(8,128)S(1)} %bitcast.12), kind=kLoop, calls=%fused_computation.2 | loop fusion | flops 24320 | bytes 5760 | tf_op jit(solution)/shard_map/reduce_sum | solution.py:696
  61.8 0.8 %slice_reduce_fusion = bf16[32,1792]{1,0:T(8,128)(2,1)} fusion(bf16[8,32,1920]{2,1,0:T(8,128)(2,1)S(1)} %all-to-all-done), kind=kLoop, calls=%fused_computation | loop fusion | flops 401408 | bytes 1032192 | tf_op jit(solution)/shard_map/reduce_sum | solution.py:692
  (2 shorter events, 0.0 us)
Async XLA Ops:
  41.9 19.2 %copy-start = (s32[32,8]{0,1:T(8,128)S(1)}, s32[32,8]{0,1:T(8,128)}, u32[]{:S(2)}) copy-start(s32[32,8]{0,1:T(8,128)} %param.12) | copy-start | bytes 3076
  41.9 19.1 %all-to-all-start = ((bf16[8,32,1920]{2,1,0:T(8,128)(2,1)}), bf16[8,32,1920]{2,1,0:T(8,128)(2,1)S(1)}, u32[]{:S(2)}, u32[]{:S(2)}) async-start(bf16[8,32,1920]{2,1,0:T(8,128)(2,1)} %get-tuple-element.14), calls=%async_computation | async-start | bytes 1966080 | tf_op jit(solution)/shard_map/all_to_all | solution.py:690
